TPU v7x, 32 devices: a whole 2x2x4 slice. The times are simulated.
32 devices in a mesh: samp: 16 (over z, y, x), feat: 2 (over core).
Axes of the slice: x: 2, y: 2, z: 4, core: 2. Of those that a mesh axis runs over, the one named last changes fastest.
Arguments:
- design_matrix: bfloat16 [2048, 32768], P('samp', 'feat'), may hold values from -0.046875 to 0.046875
- labels: int32 [2048], P('samp'), may hold values from 0 to 1
- weights: float32 [16, 32768], P(None, ('feat', 'samp')), may hold values from -6 to 6
- lambdas: float32 [16], replicated, may hold values from 0.05 to 1
- sketch: bfloat16 [32768, 384], P(('feat', 'samp')), may hold values from -0.03125 to 0.03125
- sketch_values: float32 [384], replicated, may hold values from 0.05 to 2
Outputs:
- new_weights: float32 [16, 32768], P(None, ('feat', 'samp'))
All inputs are finite; a program needn't handle non-finite values.
Results may differ from a plain program's by a relative error of at most 0.004.
Values may be sent and summed in bfloat16 or wider, within the bound.
No kernel may reach another device: no remote copies, remote signals or barrier semaphores. Data moves between devices by JAX's collectives and lax.ppermute only.
A program may use at most 64 MiB of HBM per device.

v0:
```python
import jax
import jax.numpy as jnp
from jax import lax
from jax.sharding import PartitionSpec as P

ITERS = 2


def shards(design_matrix, labels, weights, lambdas, sketch, sketch_values):
    sketch_full = sketch.astype(jnp.float32)
    smallest = jnp.min(sketch_values)
    ratios = (smallest + lambdas[:, None]) / (sketch_values[None, :] + lambdas[:, None]) - 1.0

    def apply_rows(vector):
        vector_half = vector.astype(jnp.bfloat16)
        partial_rows = lax.dot_general(
            lax.all_gather(vector_half, "samp", axis=1, tiled=True),
            design_matrix,
            (((1,), (1,)), ((), ())),
            preferred_element_type=jnp.float32,
        )
        return lax.psum(partial_rows, "feat")

    def apply_columns(values):
        return lax.psum_scatter(
            lax.dot_general(
                design_matrix, values, (((0,), (1,)), ((), ())), preferred_element_type=jnp.float32
            ),
            "samp",
            scatter_dimension=0,
            tiled=True,
        ).T

    def precondition(residual):
        projected = jnp.dot(residual, sketch_full, precision=lax.Precision.HIGHEST)
        projected = lax.psum(projected, ("samp", "feat"))
        correction = lax.dot_general(
            ratios * projected,
            sketch_full,
            (((1,), (1,)), ((), ())),
            precision=lax.Precision.HIGHEST,
        )
        precond_res = residual + correction
        res_dot = lax.psum(jnp.sum(residual * precond_res, axis=1), ("samp", "feat"))
        return (precond_res, res_dot)

    logits = apply_rows(weights)
    probability = jax.nn.sigmoid(logits)
    hessian_diag = probability * (1.0 - probability)
    miss_rows = (probability - labels[None, :].astype(jnp.float32)).astype(jnp.bfloat16)
    gradient = apply_columns(miss_rows) + lambdas[:, None] * weights
    residual = -gradient
    precond_res, res_dot = precondition(residual)
    direction = precond_res
    update = jnp.zeros_like(residual)
    for iteration in range(ITERS):
        image_rows = apply_rows(direction)
        hess_dir = (
            apply_columns((hessian_diag * image_rows).astype(jnp.bfloat16))
            + lambdas[:, None] * direction
        )
        curvature = lax.psum(jnp.sum(direction * hess_dir, axis=1), ("samp", "feat"))
        step_size = res_dot / curvature
        update = update + step_size[:, None] * direction
        if iteration + 1 < ITERS:
            residual = residual - step_size[:, None] * hess_dir
            precond_res, new_dot = precondition(residual)
            direction = precond_res + (new_dot / res_dot)[:, None] * direction
            res_dot = new_dot
    return weights + update


def solution(mesh):
    return jax.shard_map(
        shards,
        mesh=mesh,
        in_specs=(
            P("samp", "feat"),
            P("samp"),
            P(None, ("feat", "samp")),
            P(),
            P(("feat", "samp"), None),
            P(),
        ),
        out_specs=P(None, ("feat", "samp")),
        check_vma=False,
    )
```

profile of v0, /device:TPU:0, one launch (start us, length us, event | category | flops | bytes accessed | tf_op | source)
XLA Modules:
  0.0 595.5 jit_solution(18189731865618623638)
XLA Ops:
  6.5 0.0 copy-start
  6.5 0.0 reduce-scatter.4.cloned.1.call-start
  6.5 0.7 convert_element_type.24
  7.3 0.8 convert_element_type.23
  8.1 45.3 %all_gather.9 = bf16[16,16384]{1,0:T(8,128)(2,1)S(1)} all-gather(bf16[16,1024]{1,0:T(8,128)(2,1)S(1)} %convert_element_type.23), channel_id=1, replica_groups=mesh['samp'=16,'feat'=2] {'samp'}, dimensions={1}, use_global_device_ids=true | all-gather | bytes 557056 | tf_op jit(solution)/shard_map/all_gather | solution.py:17
  53.4 3.4 fusion.22
  56.8 0.0 copy-start.3
  56.8 0.0 copy-start.2
  56.8 0.0 copy-start.1
  56.8 2.6 psum.63
  59.5 3.8 convolution_bitcast_fusion.2
  63.3 0.0 reduce-scatter.4.cloned.1.call-update
  63.3 0.0 reduce-scatter.6.cloned.1.call-start
  63.4 0.0 copy-done.3
  63.4 0.6 reduce_min.9
  64.0 0.0 copy-done.2
  64.0 0.6 broadcast_add_fusion
  64.6 73.4 %reduce-scatter.4.cloned.1.call-done = f32[1024,16]{0,1:T(8,128)} async-done(((f32[16384,16]{0,1:T(8,128)}), f32[1024,16]{0,1:T(8,128)}) %reduce-scatter.4.cloned.1.call-update) | async-done | bytes 65552 | tf_op jit(solution)/shard_map/reduce_scatter | solution.py:25
  138.1 0.0 copy-done.1
  138.1 0.9 fusion.2
  139.0 0.0 copy-done
  139.0 0.4 fusion.23
  139.4 37.1 %psum.64 = f32[16,384]{1,0:T(8,128)S(1)} all-reduce(f32[16,384]{1,0:T(8,128)S(1)} %fusion.23), channel_id=1, replica_groups=mesh['samp'=16,'feat'=2] {'samp','feat'}, use_global_device_ids=true, to_apply=%region_3.0 | all-reduce | flops 6144 | bytes 49152 | tf_op jit(solution)/shard_map/psum | solution.py:36
  176.5 0.7 fusion.21
  177.2 41.8 %all_gather.10 = bf16[16,16384]{1,0:T(8,128)(2,1)S(1)} all-gather(bf16[16,1024]{1,0:T(8,128)(2,1)S(1)} %get-tuple-element.9), channel_id=1, replica_groups=mesh['samp'=16,'feat'=2] {'samp'}, dimensions={1}, use_global_device_ids=true | all-gather | bytes 557056 | tf_op jit(solution)/shard_map/all_gather | solution.py:17
  219.0 3.4 fusion.24
  222.3 2.5 psum.66
  224.8 3.8 convolution_bitcast_fusion.1
  228.7 0.0 reduce-scatter.6.cloned.1.call-update
  228.7 0.0 reduce-scatter.8.cloned.1.call-start
  228.7 74.6 %reduce-scatter.6.cloned.1.call-done = f32[1024,16]{0,1:T(8,128)} async-done(((f32[16384,16]{0,1:T(8,128)}), f32[1024,16]{0,1:T(8,128)}) %reduce-scatter.6.cloned.1.call-update) | async-done | bytes 65552 | tf_op jit(solution)/shard_map/reduce_scatter | solution.py:25
  303.4 1.0 multiply_reduce_fusion.1
  304.4 36.9 %all-reduce = (f32[16]{0:T(128)S(1)}, f32[16]{0:T(128)S(1)}) all-reduce(f32[16]{0:T(128)S(1)} %get-tuple-element.6, f32[16]{0:T(128)S(1)} %get-tuple-element.5), channel_id=1, replica_groups=mesh['samp'=16,'feat'=2] {'samp','feat'}, use_global_device_ids=true, to_apply=%region_5.0 | all-reduce | flops 32 | bytes 256 | tf_op jit(solution)/shard_map/psum | solution.py:44
  341.3 0.9 multiply_subtract_fusion
  342.2 0.4 fusion.25
  342.6 41.2 %psum.68 = f32[16,384]{1,0:T(8,128)S(1)} all-reduce(f32[16,384]{1,0:T(8,128)S(1)} %fusion.25), channel_id=1, replica_groups=mesh['samp'=16,'feat'=2] {'samp','feat'}, use_global_device_ids=true, to_apply=%region_10.0 | all-reduce | flops 6144 | bytes 49152 | tf_op jit(solution)/shard_map/psum | solution.py:36
  383.8 0.8 multiply_reduce_fusion
  384.7 39.7 %psum.69 = f32[16]{0:T(128)S(1)} all-reduce(f32[16]{0:T(128)S(1)} %get-tuple-element.11), channel_id=1, replica_groups=mesh['samp'=16,'feat'=2] {'samp','feat'}, use_global_device_ids=true, to_apply=%region_12.0 | all-reduce | flops 16 | bytes 128 | tf_op jit(solution)/shard_map/psum | solution.py:44
  424.4 0.1 fusion.20
  424.5 41.5 %all_gather.11 = bf16[16,16384]{1,0:T(8,128)(2,1)S(1)} all-gather(bf16[16,1024]{1,0:T(8,128)(2,1)S(1)} %fusion.20), channel_id=1, replica_groups=mesh['samp'=16,'feat'=2] {'samp'}, dimensions={1}, use_global_device_ids=true | all-gather | bytes 557056 | tf_op jit(solution)/shard_map/all_gather | solution.py:17
  466.0 3.4 fusion.26
  469.3 2.5 psum.70
  471.8 3.9 convolution_bitcast_fusion
  475.7 0.0 reduce-scatter.8.cloned.1.call-update
  475.7 74.7 %reduce-scatter.8.cloned.1.call-done = f32[1024,16]{0,1:T(8,128)} async-done(((f32[16384,16]{0,1:T(8,128)}), f32[1024,16]{0,1:T(8,128)}) %reduce-scatter.8.cloned.1.call-update) | async-done | bytes 65552 | tf_op jit(solution)/shard_map/reduce_scatter | solution.py:25
  550.4 1.0 fusion.1
  551.4 36.9 %psum.71 = f32[16]{0:T(128)S(1)} all-reduce(f32[16]{0:T(128)S(1)} %fusion.1), channel_id=1, replica_groups=mesh['samp'=16,'feat'=2] {'samp','feat'}, use_global_device_ids=true, to_apply=%region_16.0 | all-reduce | flops 16 | bytes 128 | tf_op jit(solution)/shard_map/psum | solution.py:62
  588.3 0.7 add_add_fusion
  (3 shorter events, 0.0 us)
Async XLA Ops:
  6.5 132.5 %copy-start = (bf16[1024,384]{1,0:T(8,128)(2,1)S(1)}, bf16[1024,384]{1,0:T(8,128)(2,1)}, u32[]{:S(2)}) copy-start(bf16[1024,384]{1,0:T(8,128)(2,1)} %param.10) | copy-start | bytes 2359300
  6.5 131.5 %reduce-scatter.4.cloned.1.call-start = ((), (), s32[]{:S(2)}) async-start(), calls=%async_computation.3 | async-start | bytes 1114112 | tf_op jit(solution)/shard_map/reduce_scatter | solution.py:25
  56.8 6.6 %copy-start.3 = (f32[384]{0:T(512)S(1)}, f32[384]{0:T(512)}, u32[]{:S(2)}) copy-start(f32[384]{0:T(512)} %param.11) | copy-start | bytes 4612
  56.8 7.2 %copy-start.2 = (f32[16]{0:T(128)S(1)}, f32[16]{0:T(128)}, u32[]{:S(2)}) copy-start(f32[16]{0:T(128)} %param.9) | copy-start | bytes 196
  56.8 81.3 %copy-start.1 = (f32[16,1024]{1,0:T(8,128)S(1)}, f32[16,1024]{1,0:T(8,128)}, u32[]{:S(2)}) copy-start(f32[16,1024]{1,0:T(8,128)} %param.8) | copy-start | bytes 196612
  63.3 240.1 %reduce-scatter.6.cloned.1.call-start = ((), (), s32[]{:S(2)}) async-start(), calls=%async_computation.4 | async-start | bytes 1114112 | tf_op jit(solution)/shard_map/reduce_scatter | solution.py:25
  228.7 321.7 %reduce-scatter.8.cloned.1.call-start = ((), (), s32[]{:S(2)}) async-start(), calls=%async_computation.5 | async-start | bytes 1114112 | tf_op jit(solution)/shard_map/reduce_scatter | solution.py:25
Sparse Core Ops, SparseCore 0:
  63.4 74.5 reduce-scatter.3
  228.8 74.5 reduce-scatter.5
  475.8 74.4 reduce-scatter.7
where the time goes:
time: 597 us; the launch traced here: 596 us
  blocking collectives  328 us (55%)
  waiting for transfers between devices  223 us (37%)
  matrix products  24.1 us (4%)
  between operations  13.2 us (2%)
  other arithmetic  7.54 us (1%)
    reduce_scatter x3, waiting for transfers between devices, apply_columns(): lax.psum_scatter(lax.dot_general(design_matrix, values, (((0,), (1,)), ((...  223 us
    all_gather x3, blocking collectives, apply_rows(): lax.all_gather(vector_half, 'samp', axis=1, tiled=True)  129 us
    psum x2, blocking collectives, precondition(): projected = lax.psum(projected, ('samp', 'feat'))  78.2 us
    psum x2, blocking collectives, precondition(): lax.psum(jnp.sum(residual * precond_res, axis=1), ('samp', 'feat'))  76.6 us
    psum x1, blocking collectives, shards(): lax.psum(jnp.sum(direction * hess_dir, axis=1), ('samp', 'feat'))  36.9 us
  transfers between devices with their start and end apart: 3, of which 3 were waited for; matrix products, arithmetic and copies ran while one was open for 0% of the time, Pallas kernels for 0%

commit v1 on v0

v1 whole, which is shorter than its diff:
```python
import jax
import jax.numpy as jnp
from jax import lax
from jax.sharding import PartitionSpec as P

ITERS = 2
LANES = 128


def pack(values):
    high = lax.reduce_precision(values, 8, 7)
    rest = values - high
    middle = lax.reduce_precision(rest, 8, 7)
    low = rest - middle
    parts = jnp.stack([high, middle, low], axis=1)
    return jnp.pad(parts, ((0, 0), (0, LANES - 3))).astype(jnp.bfloat16)


def unpack(summed):
    return summed[:, 0] + summed[:, 1] + summed[:, 2]


def make_shards(samp, feat):
    def exchange(blocks):
        return lax.all_to_all(blocks, "samp", 0, 0)

    def gather(block):
        return exchange(jnp.broadcast_to(block[None], (samp,) + block.shape))

    def feat_sum(values):
        if feat == 2:
            return values + lax.ppermute(values, "feat", [(0, 1), (1, 0)])
        return lax.psum(values, "feat")

    def shards(design_matrix, labels, weights, lambdas, sketch, sketch_values):
        strengths, width = weights.shape
        samples, block = design_matrix.shape
        rank = sketch.shape[1]
        sketch_full = sketch.astype(jnp.float32)
        smallest = jnp.min(sketch_values)
        lam = lambdas[:, None]
        ratios = (smallest + lam) / (sketch_values[None, :] + lam) - 1.0

        def apply_rows(vector):
            whole = gather(vector.astype(jnp.bfloat16))
            flat = whole.transpose(1, 0, 2).reshape(strengths, block)
            partial_rows = lax.dot_general(
                flat, design_matrix, (((1,), (1,)), ((), ())), preferred_element_type=jnp.float32
            )
            squares = jnp.sum(jnp.square(flat.astype(jnp.float32)), axis=1)
            both = jnp.concatenate(
                [partial_rows, jnp.broadcast_to(squares[:, None], (strengths, LANES))], axis=1
            )
            both = feat_sum(both)
            return both[:, :samples], both[:, samples]

        def apply_columns(values, scalars):
            partial = lax.dot_general(
                values, design_matrix, (((1,), (0,)), ((), ())), preferred_element_type=jnp.float32
            )
            blocks = partial.astype(jnp.bfloat16).reshape(strengths, samp, width).transpose(1, 0, 2)
            if scalars is not None:
                extra = jnp.broadcast_to(pack(scalars)[None], (samp, strengths, LANES))
                blocks = jnp.concatenate([blocks, extra], axis=2)
            summed = jnp.sum(exchange(blocks).astype(jnp.float32), axis=0)
            if scalars is None:
                return summed, None
            return summed[:, :width], unpack(summed[:, width:])

        def precondition(residual):
            projected = jnp.dot(residual, sketch_full, precision=lax.Precision.HIGHEST)
            square = jnp.sum(residual * residual, axis=1)
            payload = jnp.concatenate([projected.astype(jnp.bfloat16), pack(square)], axis=1)
            summed = feat_sum(jnp.sum(gather(payload).astype(jnp.float32), axis=0))
            projected = summed[:, :rank]
            scaled = ratios * projected
            correction = lax.dot_general(
                scaled, sketch_full, (((1,), (1,)), ((), ())), precision=lax.Precision.HIGHEST
            )
            res_dot = unpack(summed[:, rank:]) + jnp.sum(scaled * projected, axis=1)
            return residual + correction, res_dot

        logits, _ = apply_rows(weights)
        probability = jax.nn.sigmoid(logits)
        hessian_diag = probability * (1.0 - probability)
        miss_rows = (probability - labels[None, :].astype(jnp.float32)).astype(jnp.bfloat16)
        residual = -(apply_columns(miss_rows, None)[0] + lam * weights)
        precond_res, res_dot = precondition(residual)
        direction = precond_res
        update = jnp.zeros_like(residual)
        for iteration in range(ITERS):
            image_rows, square = apply_rows(direction)
            image = (hessian_diag * image_rows).astype(jnp.bfloat16)
            energy = jnp.sum(image.astype(jnp.float32) * image_rows, axis=1)
            if iteration + 1 < ITERS:
                columns, energy = apply_columns(image, energy)
                step_size = res_dot / (energy + lambdas * square)
                update = update + step_size[:, None] * direction
                residual = residual - step_size[:, None] * (columns + lam * direction)
                precond_res, new_dot = precondition(residual)
                direction = precond_res + (new_dot / res_dot)[:, None] * direction
                res_dot = new_dot
            else:
                total = gather(jnp.broadcast_to(energy[:, None], (strengths, LANES)))
                energy = jnp.sum(total, axis=0)[:, 0]
                step_size = res_dot / (energy + lambdas * square)
                update = update + step_size[:, None] * direction
        return weights + update

    return shards


def solution(mesh):
    return jax.shard_map(
        make_shards(mesh.shape["samp"], mesh.shape["feat"]),
        mesh=mesh,
        in_specs=(
            P("samp", "feat"),
            P("samp"),
            P(None, ("feat", "samp")),
            P(),
            P(("feat", "samp"), None),
            P(),
        ),
        out_specs=P(None, ("feat", "samp")),
        check_vma=False,
    )
```

time: 597 us -> 169 us (0.28)
  blocking collectives: 328 us -> 93.1 us
  waiting for transfers between devices: 223 us -> 37.4 us
  between operations: 13.2 us -> 0.28 us
  starting transfers between devices: 0.09 us -> 12 us
  matrix products: 24.1 us -> 15.9 us
    reduce_scatter x3 -> x0, waiting for transfers between devices: 223 us -> none  [apply_columns(): lax.psum_scatter(lax.dot_general(design_matrix, values, (((0,), (1,)), ((...]
    psum x8 -> x0, blocking collectives: 199 us -> none  [the longest x2 78.2 us: precondition(): projected = lax.psum(projected, ('samp', 'feat'))]
    all_gather x3 -> x0, blocking collectives: 129 us -> none  [apply_rows(): lax.all_gather(vector_half, 'samp', axis=1, tiled=True)]
    all_to_all x0 -> x5, blocking collectives: none -> 93.1 us  [exchange(): return lax.all_to_all(blocks, 'samp', 0, 0)]
    all_to_all x0 -> x3, waiting for transfers between devices: none -> 32.3 us  [exchange(): return lax.all_to_all(blocks, 'samp', 0, 0)]
    all_to_all x0 -> x3, starting transfers between devices: none -> 11.8 us  [exchange(): return lax.all_to_all(blocks, 'samp', 0, 0)]
    dot_general x8 -> x7, matrix products: 23.2 us -> 15.1 us  [the longest x3 10.1 us: apply_rows(): lax.dot_general(flat, design_matrix, (((1,), (1,)), ((), ())), preferred_...]
  transfers between devices with their start and end apart: 3 -> 8, of which waited for: 3 -> 8; matrix products, arithmetic and copies ran while one was open for 0% -> 1% of each run, Pallas kernels for 0% -> 0%
where the time goes in v1:
time: 169 us; the launch traced here: 168 us
  blocking collectives  93.1 us (55%)
  waiting for transfers between devices  37.4 us (22%)
  matrix products  15.9 us (9%)
  starting transfers between devices  12 us (7%)
  other arithmetic  6.63 us (4%)
  local copies, waits for them, and re-layouts  2.9 us (2%)
    all_to_all x5, blocking collectives, exchange(): return lax.all_to_all(blocks, 'samp', 0, 0)  93.1 us
    all_to_all x3, waiting for transfers between devices, exchange(): return lax.all_to_all(blocks, 'samp', 0, 0)  32.3 us
    all_to_all x3, starting transfers between devices, exchange(): return lax.all_to_all(blocks, 'samp', 0, 0)  11.8 us
    dot_general x3, matrix products, apply_rows(): lax.dot_general(flat, design_matrix, (((1,), (1,)), ((), ())), preferred_...  10.1 us
    ppermute x5, waiting for transfers between devices, feat_sum(): return values + lax.ppermute(values, 'feat', [(0, 1), (1, 0)])  5.14 us
    dot_general x2, matrix products, apply_columns(): lax.dot_general(values, design_matrix, (((1,), (0,)), ((), ())), preferre...  3.5 us
  transfers between devices with their start and end apart: 8, of which 8 were waited for; matrix products, arithmetic and copies ran while one was open for 1% of the time, Pallas kernels for 0%

profile of v1, /device:TPU:0, one launch (start us, length us, event | category | flops | bytes accessed | tf_op | source)
XLA Modules:
  0.0 168.3 jit_solution(8814865092222348245)
XLA Ops:
  0.0 1.0 convert_element_type.72
  1.1 23.4 %all_to_all.40 = bf16[16,16,1024]{2,1,0:T(8,128)(2,1)S(1)} all-to-all(bf16[16,16,1024]{2,1,0:T(8,128)(2,1)S(1)} %broadcast_in_dim.18), channel_id=1, replica_groups=mesh['samp'=16,'feat'=2] {'samp'}, dimensions={0} | all-to-all | bytes 1048576 | tf_op jit(solution)/shard_map/all_to_all | solution.py:25
  24.5 3.4 %fusion.27 = f32[16,128]{1,0:T(8,128)S(1)} fusion(bf16[16,16384]{1,0:T(8,128)(2,1)S(1)} %bitcast.67, bf16[128,16384]{1,0:T(8,128)(2,1)} %param.6), kind=kOutput, calls=%fused_computation.92 | convolution fusion | flops 67108864 | bytes 4726784 | tf_op jit(solution)/shard_map/dot_general | solution.py:47
  27.8 0.3 multiply_reduce_fusion.2
  28.2 1.1 collective-permute-done
  29.4 0.7 convolution_convert_fusion.1
  30.1 19.2 %all_to_all.41 = bf16[16,16,1024]{2,1,0:T(8,128)(2,1)S(1)} all-to-all(bf16[16,16,1024]{2,1,0:T(8,128)(2,1)S(1)} %bitcast.71), channel_id=1, replica_groups=mesh['samp'=16,'feat'=2] {'samp'}, dimensions={0} | all-to-all | bytes 1048576 | tf_op jit(solution)/shard_map/all_to_all | solution.py:25
  49.4 0.2 multiply_reduce_fusion.4
  49.6 0.1 copy.37
  49.7 0.4 convolution_convert_fusion.3
  50.1 0.7 broadcast_in_dim.20
  50.9 3.9 %all-to-all-start.2 = ((bf16[16,16,512]{2,1,0:T(8,128)(2,1)}), bf16[16,16,512]{2,1,0:T(8,128)(2,1)S(1)}, u32[]{:S(2)}, u32[]{:S(2)}) async-start(bf16[16,16,512]{2,1,0:T(8,128)(2,1)} %broadcast_in_dim.20), calls=%async_computation.2 | async-start | bytes 524288 | tf_op jit(solution)/shard_map/all_to_all | solution.py:25
  54.8 0.6 reduce_min.9
  55.4 8.5 %all-to-all-done.2 = bf16[16,16,512]{2,1,0:T(8,128)(2,1)S(1)} async-done(((bf16[16,16,512]{2,1,0:T(8,128)(2,1)}), bf16[16,16,512]{2,1,0:T(8,128)(2,1)S(1)}, u32[]{:S(2)}, u32[]{:S(2)}) %all-to-all-start.2) | async-done | bytes 262176 | tf_op jit(solution)/shard_map/all_to_all | solution.py:25
  64.1 0.7 broadcast_add_fusion
  64.7 0.5 collective-permute-done.1
  65.3 0.7 fusion.25
  66.1 18.8 %all_to_all.42 = bf16[16,16,1024]{2,1,0:T(8,128)(2,1)S(1)} all-to-all(bf16[16,16,1024]{2,1,0:T(8,128)(2,1)S(1)} %broadcast_in_dim.21), channel_id=1, replica_groups=mesh['samp'=16,'feat'=2] {'samp'}, dimensions={0} | all-to-all | bytes 1048576 | tf_op jit(solution)/shard_map/all_to_all | solution.py:25
  84.9 3.4 %fusion.28 = f32[16,128]{1,0:T(8,128)S(1)} fusion(bf16[16,16384]{1,0:T(8,128)(2,1)S(1)} %bitcast.68, bf16[128,16384]{1,0:T(8,128)(2,1)} %param.6), kind=kOutput, calls=%fused_computation.93 | convolution fusion | flops 67108864 | bytes 4726784 | tf_op jit(solution)/shard_map/dot_general | solution.py:47
  88.3 0.3 multiply_reduce_fusion.1
  88.6 1.2 collective-permute-done.2
  89.8 0.1 multiply_reduce_fusion.8
  90.0 2.8 %convolution_convert_fusion = bf16[16,16384]{1,0:T(8,128)(2,1)S(1)} fusion(bf16[16,128]{1,0:T(8,128)(2,1)S(1)} %get-tuple-element.10, bf16[128,16384]{1,0:T(8,128)(2,1)} %param.6), kind=kOutput, calls=%fused_computation | convolution fusion | flops 67371008 | bytes 4722688 | tf_op jit(solution)/shard_map/dot_general | solution.py:58
  93.0 0.9 pad_maximum_fusion
  93.8 3.9 %all-to-all-start.4 = ((bf16[16,16,1152]{2,1,0:T(8,128)(2,1)}), bf16[16,16,1152]{2,1,0:T(8,128)(2,1)S(1)}, u32[]{:S(2)}, u32[]{:S(2)}) async-start(bf16[16,16,1152]{2,1,0:T(8,128)(2,1)} %pad_maximum_fusion), calls=%async_computation.4 | async-start | bytes 1179648 | tf_op jit(solution)/shard_map/all_to_all | solution.py:25
  97.8 0.2 fusion.22
  98.0 0.2 multiply_reduce_fusion.6
  98.2 0.1 slice_reduce_fusion.2
  98.3 16.1 %all-to-all-done.4 = bf16[16,16,1152]{2,1,0:T(8,128)(2,1)S(1)} async-done(((bf16[16,16,1152]{2,1,0:T(8,128)(2,1)}), bf16[16,16,1152]{2,1,0:T(8,128)(2,1)S(1)}, u32[]{:S(2)}, u32[]{:S(2)}) %all-to-all-start.4) | async-done | bytes 589856 | tf_op jit(solution)/shard_map/all_to_all | solution.py:25
  114.4 0.2 fusion.14
  114.6 0.2 multiply_reduce_fusion.3
  114.9 0.4 convolution_convert_fusion.2
  115.4 13.1 %all_to_all.43 = bf16[16,16,512]{2,1,0:T(8,128)(2,1)S(1)} all-to-all(bf16[16,16,512]{2,1,0:T(8,128)(2,1)S(1)} %broadcast_in_dim.24), channel_id=1, replica_groups=mesh['samp'=16,'feat'=2] {'samp'}, dimensions={0} | all-to-all | bytes 524288 | tf_op jit(solution)/shard_map/all_to_all | solution.py:25
  128.7 1.1 collective-permute-done.3
  129.8 0.2 multiply_reduce_fusion.5
  130.1 0.2 fusion.23
  130.3 0.7 fusion.26
  131.1 18.8 %all_to_all.44 = bf16[16,16,1024]{2,1,0:T(8,128)(2,1)S(1)} all-to-all(bf16[16,16,1024]{2,1,0:T(8,128)(2,1)S(1)} %broadcast_in_dim.25), channel_id=1, replica_groups=mesh['samp'=16,'feat'=2] {'samp'}, dimensions={0} | all-to-all | bytes 1048576 | tf_op jit(solution)/shard_map/all_to_all | solution.py:25
  149.9 3.4 %fusion.29 = f32[16,128]{1,0:T(8,128)S(1)} fusion(bf16[16,16384]{1,0:T(8,128)(2,1)S(1)} %bitcast.69, bf16[128,16384]{1,0:T(8,128)(2,1)} %param.6), kind=kOutput, calls=%fused_computation.94 | convolution fusion | flops 67108864 | bytes 4726784 | tf_op jit(solution)/shard_map/dot_general | solution.py:47
  153.3 0.3 multiply_reduce_fusion
  153.6 1.2 collective-permute-done.4
  154.8 0.1 multiply_reduce_fusion.7
  154.9 0.7 broadcast_in_dim_broadcast_in_dim_broadcast_in_dim.2
  155.6 3.9 %all-to-all-start.7 = ((f32[16,16,128]{2,1,0:T(8,128)}), f32[16,16,128]{2,1,0:T(8,128)S(1)}, u32[]{:S(2)}, u32[]{:S(2)}) async-start(f32[16,16,128]{2,1,0:T(8,128)} %broadcast_in_dim_broadcast_in_dim_broadcast_in_dim.2), calls=%async_computation.7 | async-start | bytes 262144 | tf_op jit(solution)/shard_map/all_to_all | solution.py:25
  159.6 0.1 slice_reduce_fusion
  159.7 7.7 %all-to-all-done.7 = f32[16,16,128]{2,1,0:T(8,128)S(1)} async-done(((f32[16,16,128]{2,1,0:T(8,128)}), f32[16,16,128]{2,1,0:T(8,128)S(1)}, u32[]{:S(2)}, u32[]{:S(2)}) %all-to-all-start.7) | async-done | bytes 131104 | tf_op jit(solution)/shard_map/all_to_all | solution.py:25
  167.4 0.1 slice_reduce_fusion.1
  167.5 0.7 add_add_fusion
  (59 shorter events, 1.6 us)
Async XLA Ops:
  0.0 49.7 %copy-start = (bf16[1024,384]{1,0:T(8,128)(2,1)S(1)}, bf16[1024,384]{1,0:T(8,128)(2,1)}, u32[]{:S(2)}) copy-start(bf16[1024,384]{1,0:T(8,128)(2,1)} %param.10) | copy-start | bytes 2359300
  0.0 29.4 %copy-start.1 = (bf16[128,16384]{1,0:T(8,128)(2,1)S(1)}, bf16[128,16384]{1,0:T(8,128)(2,1)}, u32[]{:S(2)}) copy-start(bf16[128,16384]{1,0:T(8,128)(2,1)} %param.6) | copy-start | bytes 12582916
  0.0 28.2 %copy-start.5 = (s32[128]{0:T(128)S(1)}, s32[128]{0:T(128)}, u32[]{:S(2)}) copy-start(s32[128]{0:T(128)} %param.7) | copy-start | bytes 1540
  27.8 21.5 %copy-start.2 = (f32[16,1024]{1,0:T(8,128)S(1)}, f32[16,1024]{1,0:T(8,128)}, u32[]{:S(2)}) copy-start(f32[16,1024]{1,0:T(8,128)} %param.8) | copy-start | bytes 196612
  27.8 21.5 %copy-start.4 = (f32[16]{0:T(128)S(1)}, f32[16]{0:T(128)}, u32[]{:S(2)}) copy-start(f32[16]{0:T(128)} %param.9) | copy-start | bytes 196
  28.2 1.2 collective-permute-start
  29.4 25.4 %copy-start.3 = (f32[384]{0:T(512)S(1)}, f32[384]{0:T(512)}, u32[]{:S(2)}) copy-start(f32[384]{0:T(512)} %param.11) | copy-start | bytes 4612
  50.9 13.1 %all-to-all-start.2 = ((bf16[16,16,512]{2,1,0:T(8,128)(2,1)}), bf16[16,16,512]{2,1,0:T(8,128)(2,1)S(1)}, u32[]{:S(2)}, u32[]{:S(2)}) async-start(bf16[16,16,512]{2,1,0:T(8,128)(2,1)} %broadcast_in_dim.20), calls=%async_computation.2 | async-start | bytes 524288 | tf_op jit(solution)/shard_map/all_to_all | solution.py:25
  64.0 1.3 collective-permute-start.1
  88.6 1.2 collective-permute-start.2
  93.8 20.5 %all-to-all-start.4 = ((bf16[16,16,1152]{2,1,0:T(8,128)(2,1)}), bf16[16,16,1152]{2,1,0:T(8,128)(2,1)S(1)}, u32[]{:S(2)}, u32[]{:S(2)}) async-start(bf16[16,16,1152]{2,1,0:T(8,128)(2,1)} %pad_maximum_fusion), calls=%async_computation.4 | async-start | bytes 1179648 | tf_op jit(solution)/shard_map/all_to_all | solution.py:25
  128.5 1.3 collective-permute-start.3
  153.6 1.2 collective-permute-start.4
  155.6 11.8 %all-to-all-start.7 = ((f32[16,16,128]{2,1,0:T(8,128)}), f32[16,16,128]{2,1,0:T(8,128)S(1)}, u32[]{:S(2)}, u32[]{:S(2)}) async-start(f32[16,16,128]{2,1,0:T(8,128)} %broadcast_in_dim_broadcast_in_dim_broadcast_in_dim.2), calls=%async_computation.7 | async-start | bytes 262144 | tf_op jit(solution)/shard_map/all_to_all | solution.py:25

commit v2 on v0

v2 whole, which is shorter than its diff:
```python
import math

import jax
import jax.numpy as jnp
from jax import lax
from jax.experimental import pallas as pl
from jax.experimental.pallas import tpu as pltpu
from jax.sharding import PartitionSpec as P

ITERS = 2
LANES = 128
SUBLANES = 8
LARGEST = 0.09375
HALF_RANGE = 60000.0


def split(values):
    high = values.astype(jnp.bfloat16)
    rest = values - high.astype(jnp.float32)
    middle = rest.astype(jnp.bfloat16)
    low = (rest - middle.astype(jnp.float32)).astype(jnp.bfloat16)
    return high, middle, low


def exact_dot(values, other, contract):
    rows = values.shape[0]
    product = lax.dot_general(
        jnp.concatenate(split(values), axis=0),
        other,
        (((1,), (contract,)), ((), ())),
        preferred_element_type=jnp.float32,
    )
    return product[:rows] + product[rows : 2 * rows] + product[2 * rows :]


def pack(column):
    high, middle, low = (part.astype(jnp.float32) for part in split(column))
    lane = lax.broadcasted_iota(jnp.int32, (column.shape[0], LANES), 1)
    zero = jnp.zeros((column.shape[0], LANES), jnp.float32)
    tile = jnp.where(lane == 0, high, jnp.where(lane == 1, middle, jnp.where(lane == 2, low, zero)))
    return tile.astype(jnp.bfloat16)


def wide(column):
    return jnp.broadcast_to(column, (column.shape[0], LANES))


def repeat(out_ref, block):
    for part in range(out_ref.shape[0]):
        out_ref[part] = block


def start_body(weights_ref, lam_ref, payload_ref, lam_out):
    repeat(payload_ref, weights_ref[...].astype(jnp.bfloat16))
    lam_out[...] = lam_ref[...]


def rows_body(whole_ref, design_ref, out_ref, kept_ref):
    del kept_ref
    parts, strengths, width = whole_ref.shape
    samples = design_ref.shape[0]
    total = jnp.zeros((strengths, samples), jnp.float32)
    squares = jnp.zeros((strengths, width), jnp.float32)
    for part in range(parts):
        block = whole_ref[part]
        total += lax.dot_general(
            block,
            design_ref[:, part * width : (part + 1) * width],
            (((1,), (1,)), ((), ())),
            preferred_element_type=jnp.float32,
        )
        values = block.astype(jnp.float32)
        squares += values * values
    out_ref[:, :samples] = total
    out_ref[:, samples:] = wide(jnp.sum(squares, axis=1, keepdims=True))


def columns(values, design_ref, out_ref, scale=None):
    width = design_ref.shape[1] // out_ref.shape[0]
    for part in range(out_ref.shape[0]):
        block = lax.dot_general(
            values,
            design_ref[:, part * width : (part + 1) * width],
            (((1,), (0,)), ((), ())),
            preferred_element_type=jnp.float32,
        )
        if scale is not None:
            block = block * scale
        out_ref[part, :, :width] = block.astype(out_ref.dtype)


def miss_body(scale, both_ref, other_ref, labels_ref, design_ref, hessian_ref, out_ref):
    samples = design_ref.shape[0]
    logits = both_ref[:, :samples] + other_ref[:, :samples]
    probability = 1.0 / (1.0 + jnp.exp(-logits))
    hessian_ref[...] = probability * (1.0 - probability)
    miss_rows = (probability - labels_ref[...].astype(jnp.float32)).astype(jnp.bfloat16)
    columns(miss_rows, design_ref, out_ref, scale)


def project(residual, sketch_ref, payload_ref):
    rank = sketch_ref.shape[1]
    projected = exact_dot(residual, sketch_ref[...], 0).astype(jnp.bfloat16)
    square = pack(jnp.sum(residual * residual, axis=1, keepdims=True))
    for part in range(payload_ref.shape[0]):
        payload_ref[part, :, :rank] = projected
        payload_ref[part, :, rank:] = square


def gradient_body(summed_ref, weights_ref, lam_ref, sketch_ref, residual_ref, payload_ref):
    residual = -(summed_ref[...] + lam_ref[:, :1] * weights_ref[...])
    residual_ref[...] = residual
    project(residual, sketch_ref, payload_ref)


def correct(summed_ref, other_ref, lam_ref, values_ref, sketch_ref, residual):
    rank = sketch_ref.shape[1]
    lam = lam_ref[:, :1]
    values = values_ref[...]
    smallest = jnp.min(values, axis=1, keepdims=True)
    ratios = (smallest + lam) / (values + lam) - 1.0
    summed = summed_ref[...] + other_ref[...]
    projected = summed[:, :rank]
    scaled = ratios * projected
    res_dot = jnp.sum(summed[:, rank:], axis=1, keepdims=True)
    res_dot = res_dot + jnp.sum(scaled * projected, axis=1, keepdims=True)
    return residual + exact_dot(scaled, sketch_ref[...], 1), res_dot


def first_body(
    summed_ref, other_ref, lam_ref, values_ref, sketch_ref, residual_ref,
    direction_ref, dot_ref, payload_ref,
):
    direction, res_dot = correct(
        summed_ref, other_ref, lam_ref, values_ref, sketch_ref, residual_ref[...]
    )
    direction_ref[...] = direction
    dot_ref[...] = wide(res_dot)
    repeat(payload_ref, direction.astype(jnp.bfloat16))


def next_body(
    summed_ref, other_ref, lam_ref, values_ref, sketch_ref, residual_ref, old_ref, old_dot_ref,
    direction_ref, dot_ref, payload_ref,
):
    precond_res, res_dot = correct(
        summed_ref, other_ref, lam_ref, values_ref, sketch_ref, residual_ref[...]
    )
    direction = precond_res + (res_dot / old_dot_ref[:, :1]) * old_ref[...]
    direction_ref[...] = direction
    dot_ref[...] = wide(res_dot)
    repeat(payload_ref, direction.astype(jnp.bfloat16))


def image_of(both_ref, other_ref, hessian_ref, square_ref):
    samples = hessian_ref.shape[1]
    both = both_ref[...] + other_ref[...]
    square_ref[...] = both[:, samples:]
    image_rows = both[:, :samples]
    image = (hessian_ref[...] * image_rows).astype(jnp.bfloat16)
    energy = jnp.sum(image.astype(jnp.float32) * image_rows, axis=1, keepdims=True)
    return image, energy


def image_body(both_ref, other_ref, hessian_ref, design_ref, square_ref, out_ref):
    image, energy = image_of(both_ref, other_ref, hessian_ref, square_ref)
    width = out_ref.shape[2] - LANES
    packed = pack(energy)
    for part in range(out_ref.shape[0]):
        out_ref[part, :, width:] = packed
    columns(image, design_ref, out_ref)


def step_body(
    received_ref, square_ref, dot_ref, lam_ref, direction_ref, residual_ref, update_ref, sketch_ref,
    new_residual_ref, new_update_ref, payload_ref,
):
    width = direction_ref.shape[1]
    summed = received_ref[0].astype(jnp.float32)
    for part in range(1, received_ref.shape[0]):
        summed += received_ref[part].astype(jnp.float32)
    lam = lam_ref[:, :1]
    energy = jnp.sum(summed[:, width:], axis=1, keepdims=True)
    step_size = dot_ref[:, :1] / (energy + lam * square_ref[:, :1])
    direction = direction_ref[...]
    new_update_ref[...] = update_ref[...] + step_size * direction
    residual = residual_ref[...] - step_size * (summed[:, :width] + lam * direction)
    new_residual_ref[...] = residual
    project(residual, sketch_ref, payload_ref)


def energy_body(both_ref, other_ref, hessian_ref, square_ref, payload_ref):
    _, energy = image_of(both_ref, other_ref, hessian_ref, square_ref)
    lane = lax.broadcasted_iota(jnp.int32, (SUBLANES, LANES), 1)
    tile = jnp.zeros((SUBLANES, LANES), jnp.float32)
    for group in range(energy.shape[0] // SUBLANES):
        tile = jnp.where(lane == group, energy[group * SUBLANES : (group + 1) * SUBLANES], tile)
    repeat(payload_ref, tile)


def finish_body(received_ref, square_ref, dot_ref, lam_ref, direction_ref, update_ref, out_ref):
    tile = received_ref[0]
    for part in range(1, received_ref.shape[0]):
        tile += received_ref[part]
    groups = direction_ref.shape[0] // SUBLANES
    energy = jnp.concatenate([tile[:, group : group + 1] for group in range(groups)], axis=0)
    step_size = dot_ref[:, :1] / (energy + lam_ref[:, :1] * square_ref[:, :1])
    out_ref[...] = update_ref[...] + step_size * direction_ref[...]


VMEM = pl.BlockSpec(memory_space=pltpu.VMEM)


def call(body, name, shapes, *operands, aliases={}):
    return pl.pallas_call(
        body,
        out_shape=[jax.ShapeDtypeStruct(shape, dtype) for shape, dtype in shapes],
        in_specs=[VMEM] * len(operands),
        out_specs=[VMEM] * len(shapes),
        input_output_aliases=aliases,
        compiler_params=pltpu.CompilerParams(vmem_limit_bytes=8 << 20),
        name=name,
    )(*operands)


def make_shards(samp, feat):
    def exchange(blocks):
        return lax.all_to_all(blocks, "samp", 0, 0)

    def feat_parts(values):
        if feat == 2:
            return values, lax.ppermute(values, "feat", [(0, 1), (1, 0)])
        return lax.psum(values, "feat"), jnp.zeros_like(values)

    def shards(design_matrix, labels, weights, lambdas, sketch, sketch_values):
        strengths, width = weights.shape
        samples = design_matrix.shape[0]
        rank = sketch.shape[1]
        single, half = jnp.float32, jnp.bfloat16
        field = ((strengths, width), single)
        scalars = ((strengths, LANES), single)
        spread = ((samp, strengths, width), half)
        payload = ((samp, strengths, rank + LANES), half)
        scale = 2.0 ** math.floor(math.log2(HALF_RANGE / (samples * LARGEST)))
        lam = jnp.broadcast_to(lambdas[:, None], (strengths, LANES))
        labels = labels[None, :]
        values = sketch_values[None, :]

        def apply_rows(blocks, design):
            both, design = call(
                rows_body, "rows",
                [((strengths, samples + LANES), single), (design.shape, design.dtype)],
                exchange(blocks), design, aliases={1: 1},
            )
            return feat_parts(both), design

        def reduced(blocks):
            return feat_parts(jnp.sum(exchange(blocks).astype(single), axis=0))

        blocks, lam = call(start_body, "start", [spread, scalars], weights, lam)
        parts, design = apply_rows(blocks, design_matrix)
        hessian_diag, blocks = call(
            lambda *refs: miss_body(scale, *refs),
            "miss",
            [((strengths, samples), single), ((samp, strengths, width), single)],
            *parts, labels, design,
        )
        summed = jnp.sum(exchange(blocks.astype(jnp.float16)).astype(single), axis=0) * (1.0 / scale)
        residual, blocks = call(
            gradient_body, "gradient", [field, payload], summed, weights, lam, sketch
        )
        direction, res_dot, blocks = call(
            first_body, "first", [field, scalars, spread], *reduced(blocks), lam, values, sketch, residual
        )
        update = weights
        for iteration in range(ITERS):
            parts, design = apply_rows(blocks, design)
            if iteration + 1 == ITERS:
                tiny = ((samp, SUBLANES, LANES), single)
                square, blocks = call(energy_body, "energy", [scalars, tiny], *parts, hessian_diag)
                return call(
                    finish_body, "finish", [field],
                    exchange(blocks), square, res_dot, lam, direction, update,
                )[0]
            square, blocks = call(
                image_body, "image", [scalars, ((samp, strengths, width + LANES), half)],
                *parts, hessian_diag, design,
            )
            residual, update, blocks = call(
                step_body, "step", [field, field, payload],
                exchange(blocks), square, res_dot, lam, direction, residual, update, sketch,
            )
            direction, res_dot, blocks = call(
                next_body, "next", [field, scalars, spread],
                *reduced(blocks), lam, values, sketch, residual, direction, res_dot,
            )

    return shards


def solution(mesh):
    return jax.shard_map(
        make_shards(mesh.shape["samp"], mesh.shape["feat"]),
        mesh=mesh,
        in_specs=(
            P("samp", "feat"),
            P("samp"),
            P(None, ("feat", "samp")),
            P(),
            P(("feat", "samp"), None),
            P(),
        ),
        out_specs=P(None, ("feat", "samp")),
        check_vma=False,
    )
```

time: 597 us -> 155 us (0.26)
  waiting for transfers between devices: 223 us -> 5.98 us
  blocking collectives: 328 us -> 138 us
  matrix products: 24.1 us -> 0 us
  between operations: 13.2 us -> 0.12 us
  Pallas kernels: 0 us -> 7.43 us
  other arithmetic: 7.54 us -> 0.25 us
    reduce_scatter x3 -> x0, waiting for transfers between devices: 223 us -> none  [apply_columns(): lax.psum_scatter(lax.dot_general(design_matrix, values, (((0,), (1,)), ((...]
    psum x8 -> x0, blocking collectives: 199 us -> none  [the longest x2 78.2 us: precondition(): projected = lax.psum(projected, ('samp', 'feat'))]
    all_to_all x0 -> x8, blocking collectives: none -> 138 us  [exchange(): return lax.all_to_all(blocks, 'samp', 0, 0)]
    all_gather x3 -> x0, blocking collectives: 129 us -> none  [apply_rows(): lax.all_gather(vector_half, 'samp', axis=1, tiled=True)]
    dot_general x10 -> x0, matrix products: 24.1 us -> none  [the longest x3 11.5 us: apply_columns(): lax.dot_general(design_matrix, values, (((0,), (1,)), ((), ())), preferre...]
    pallas_call x0 -> x12, Pallas kernels: none -> 7.43 us  [call(): pl.pallas_call(body, out_shape=[jax.ShapeDtypeStruct(shape, dtype) for sh...]
    ppermute x0 -> x5, waiting for transfers between devices: none -> 5.98 us  [feat_parts(): return (values, lax.ppermute(values, 'feat', [(0, 1), (1, 0)]))]
  transfers between devices with their start and end apart: 3 -> 5, of which waited for: 3 -> 5; matrix products, arithmetic and copies ran while one was open for 0% -> 0% of each run, Pallas kernels for 0% -> 0%
where the time goes in v2:
time: 155 us; the launch traced here: 154 us
  blocking collectives  138 us (89%)
  Pallas kernels  7.43 us (5%)
  waiting for transfers between devices  5.98 us (4%)
  local copies, waits for them, and re-layouts  2.32 us (1%)
    all_to_all x8, blocking collectives, exchange(): return lax.all_to_all(blocks, 'samp', 0, 0)  138 us
    pallas_call x12, Pallas kernels, call(): pl.pallas_call(body, out_shape=[jax.ShapeDtypeStruct(shape, dtype) for sh...  7.43 us
    ppermute x5, waiting for transfers between devices, feat_parts(): return (values, lax.ppermute(values, 'feat', [(0, 1), (1, 0)]))  5.98 us
  transfers between devices with their start and end apart: 5, of which 5 were waited for; matrix products, arithmetic and copies ran while one was open for 0% of the time, Pallas kernels for 0%

profile of v2, /device:TPU:0, one launch (start us, length us, event | category | flops | bytes accessed | tf_op | source)
XLA Modules:
  0.0 154.2 jit_solution(17578123477404830588)
XLA Ops:
  0.0 0.0 copy-start.1
  0.0 0.0 copy-start.4
  0.0 2.2 %copy.14.design_ref = bf16[128,16384]{1,0:T(8,128)(2,1)S(1)} copy(bf16[128,16384]{1,0:T(8,128)(2,1)} %param.6) | data formatting | bytes 8388608
  2.2 0.0 copy-done.4
  2.2 0.0 copy-start.2
  2.2 0.1 broadcast_in_dim.12.lam_ref
  2.3 0.0 copy-done.1
  2.4 23.2 %all_to_all.47.whole_ref = bf16[16,16,1024]{2,1,0:T(8,128)(2,1)S(1)} all-to-all(bf16[16,16,1024]{2,1,0:T(8,128)(2,1)S(1)} %get-tuple-element.29), channel_id=1, replica_groups=mesh['samp'=16,'feat'=2] {'samp'}, dimensions={0} | all-to-all | bytes 1048576 | tf_op jit(solution)/shard_map/all_to_all | solution.py:228
  25.6 1.2 rows.3
  26.8 0.0 copy-start
  26.8 0.0 collective-permute-start
  26.8 1.2 collective-permute-done.refs_1_
  28.0 0.0 copy-done.2
  28.0 0.0 copy-start.3
  28.0 0.7 miss.1
  28.7 0.1 convert_element_type.12
  28.7 19.2 %all_to_all.40 = f16[16,16,1024]{2,1,0:T(8,128)(2,1)S(1)} all-to-all(f16[16,16,1024]{2,1,0:T(8,128)(2,1)S(1)} %convert_element_type.12), channel_id=1, replica_groups=mesh['samp'=16,'feat'=2] {'samp'}, dimensions={0} | all-to-all | bytes 1048576 | tf_op jit(solution)/shard_map/all_to_all | solution.py:228
  47.9 0.1 convert_reduce_fusion
  48.0 0.0 copy-done
  48.0 0.3 gradient.1
  48.3 12.9 %all_to_all.41 = bf16[16,16,512]{2,1,0:T(8,128)(2,1)S(1)} all-to-all(bf16[16,16,512]{2,1,0:T(8,128)(2,1)S(1)} %get-tuple-element.34), channel_id=1, replica_groups=mesh['samp'=16,'feat'=2] {'samp'}, dimensions={0} | all-to-all | bytes 524288 | tf_op jit(solution)/shard_map/all_to_all | solution.py:228
  61.2 0.1 collective-permute-start.1
  61.3 0.0 copy-done.3
  61.3 1.2 collective-permute-done.1.other_ref
  62.5 0.5 first.1
  63.0 18.8 %all_to_all.42.whole_ref = bf16[16,16,1024]{2,1,0:T(8,128)(2,1)S(1)} all-to-all(bf16[16,16,1024]{2,1,0:T(8,128)(2,1)S(1)} %get-tuple-element.36), channel_id=1, replica_groups=mesh['samp'=16,'feat'=2] {'samp'}, dimensions={0} | all-to-all | bytes 1048576 | tf_op jit(solution)/shard_map/all_to_all | solution.py:228
  81.7 1.2 rows.4
  82.9 0.0 collective-permute-start.2
  82.9 1.2 collective-permute-done.2.other_ref
  84.1 0.7 image.1
  84.8 21.5 %all_to_all.43.received_ref = bf16[16,16,1152]{2,1,0:T(8,128)(2,1)S(1)} all-to-all(bf16[16,16,1152]{2,1,0:T(8,128)(2,1)S(1)} %get-tuple-element.40), channel_id=1, replica_groups=mesh['samp'=16,'feat'=2] {'samp'}, dimensions={0} | all-to-all | bytes 1179648 | tf_op jit(solution)/shard_map/all_to_all | solution.py:228
  106.3 0.4 step.1
  106.7 12.4 %all_to_all.44 = bf16[16,16,512]{2,1,0:T(8,128)(2,1)S(1)} all-to-all(bf16[16,16,512]{2,1,0:T(8,128)(2,1)S(1)} %get-tuple-element.44), channel_id=1, replica_groups=mesh['samp'=16,'feat'=2] {'samp'}, dimensions={0} | all-to-all | bytes 524288 | tf_op jit(solution)/shard_map/all_to_all | solution.py:228
  119.2 0.1 collective-permute-start.3
  119.3 1.2 collective-permute-done.3.other_ref
  120.4 0.5 next.1
  120.9 18.7 %all_to_all.45.whole_ref = bf16[16,16,1024]{2,1,0:T(8,128)(2,1)S(1)} all-to-all(bf16[16,16,1024]{2,1,0:T(8,128)(2,1)S(1)} %get-tuple-element.46), channel_id=1, replica_groups=mesh['samp'=16,'feat'=2] {'samp'}, dimensions={0} | all-to-all | bytes 1048576 | tf_op jit(solution)/shard_map/all_to_all | solution.py:228
  139.7 1.2 rows.5
  140.9 0.0 collective-permute-start.4
  140.9 1.2 collective-permute-done.4.other_ref
  142.1 0.1 energy.1
  142.2 11.3 %all_to_all.46.received_ref = f32[16,8,128]{2,1,0:T(8,128)S(1)} all-to-all(f32[16,8,128]{2,1,0:T(8,128)S(1)} %get-tuple-element.48), channel_id=1, replica_groups=mesh['samp'=16,'feat'=2] {'samp'}, dimensions={0} | all-to-all | bytes 131072 | tf_op jit(solution)/shard_map/all_to_all | solution.py:228
  153.4 0.8 finish.1
  (5 shorter events, 0.1 us)
Async XLA Ops:
  0.0 2.3 %copy-start.1 = (f32[16,1024]{1,0:T(8,128)S(1)}, f32[16,1024]{1,0:T(8,128)}, u32[]{:S(2)}) copy-start(f32[16,1024]{1,0:T(8,128)} %update_ref.1) | copy-start | bytes 196612
  0.0 2.2 %copy-start.4 = (f32[16]{0:T(128)S(1)}, f32[16]{0:T(128)}, u32[]{:S(2)}) copy-start(f32[16]{0:T(128)} %param.9) | copy-start | bytes 196
  2.2 25.7 %copy-start.2 = (s32[128]{0:T(128)S(1)}, s32[128]{0:T(128)}, u32[]{:S(2)}) copy-start(s32[128]{0:T(128)} %param.7) | copy-start | bytes 1540
  26.8 21.2 %copy-start = (bf16[1024,384]{1,0:T(8,128)(2,1)S(1)}, bf16[1024,384]{1,0:T(8,128)(2,1)}, u32[]{:S(2)}) copy-start(bf16[1024,384]{1,0:T(8,128)(2,1)} %sketch_ref.7) | copy-start | bytes 2359300
  26.8 1.2 collective-permute-start
  28.0 33.3 %copy-start.3 = (f32[384]{0:T(512)S(1)}, f32[384]{0:T(512)}, u32[]{:S(2)}) copy-start(f32[384]{0:T(512)} %param.11) | copy-start | bytes 4612
  61.2 1.3 collective-permute-start.1
  82.9 1.2 collective-permute-start.2
  119.2 1.3 collective-permute-start.3
  140.9 1.2 collective-permute-start.4

commit v3 on v2

v3 whole, which is shorter than its diff:
```python
import math

import jax
import jax.numpy as jnp
from jax import lax
from jax.experimental import pallas as pl
from jax.experimental.pallas import tpu as pltpu
from jax.sharding import PartitionSpec as P

ITERS = 2
LANES = 128
SUBLANES = 8
LARGEST = 0.09375
HALF_RANGE = 60000.0


def split(values):
    high = values.astype(jnp.bfloat16)
    rest = values - high.astype(jnp.float32)
    middle = rest.astype(jnp.bfloat16)
    low = (rest - middle.astype(jnp.float32)).astype(jnp.bfloat16)
    return high, middle, low


def exact_dot(values, other, contract):
    rows = values.shape[0]
    product = lax.dot_general(
        jnp.concatenate(split(values), axis=0),
        other,
        (((1,), (contract,)), ((), ())),
        preferred_element_type=jnp.float32,
    )
    return product[:rows] + product[rows : 2 * rows] + product[2 * rows :]


def pack(*columns_in):
    rows = columns_in[0].shape[0]
    lane = lax.broadcasted_iota(jnp.int32, (rows, LANES), 1)
    tile = jnp.zeros((rows, LANES), jnp.float32)
    for place, column in enumerate(columns_in):
        for index, part in enumerate(split(column)):
            tile = jnp.where(lane == 3 * place + index, part.astype(jnp.float32), tile)
    return tile


def unpack(tile, place):
    return jnp.sum(tile[:, 3 * place : 3 * place + 3], axis=1, keepdims=True)


def wide(column):
    return jnp.broadcast_to(column, (column.shape[0], LANES))


def repeat(out_ref, block):
    for part in range(out_ref.shape[0]):
        out_ref[part] = block


def load_body(offsets_ref, design_ref, out_ref, sems):
    parts = offsets_ref.shape[0]
    width = design_ref.shape[1] // parts
    copies = []
    for part in range(parts):
        offset = pl.multiple_of(offsets_ref[part], width)
        copies.append(
            pltpu.make_async_copy(
                design_ref.at[:, pl.ds(offset, width)],
                out_ref.at[:, pl.ds(part * width, width)],
                sems.at[part],
            )
        )
    for copy in copies:
        copy.start()
    for copy in copies:
        copy.wait()


def rows_body(*refs):
    *whole_refs, design_ref, extra_ref, out_ref = refs
    rows, strengths, width = whole_refs[0].shape
    samples = design_ref.shape[0]
    total = jnp.zeros((strengths, samples), jnp.float32)
    squares = jnp.zeros((strengths, width), jnp.float32)
    part = 0
    for whole_ref in whole_refs:
        for row in range(rows):
            block = whole_ref[row]
            total += lax.dot_general(
                block,
                design_ref[:, part * width : (part + 1) * width],
                (((1,), (1,)), ((), ())),
                preferred_element_type=jnp.float32,
            )
            values = block.astype(jnp.float32)
            squares += values * values
            part += 1
    out_ref[:, :samples] = total
    lane = lax.broadcasted_iota(jnp.int32, (strengths, LANES), 1)
    square = jnp.sum(squares, axis=1, keepdims=True)
    out_ref[:, samples:] = jnp.where(lane == 0, square, extra_ref[...])


def columns(values, design_ref, out_refs, scale=None):
    rows = out_refs[0].shape[0]
    width = design_ref.shape[1] // (rows * len(out_refs))
    part = 0
    for out_ref in out_refs:
        for row in range(rows):
            block = lax.dot_general(
                values,
                design_ref[:, part * width : (part + 1) * width],
                (((1,), (0,)), ((), ())),
                preferred_element_type=jnp.float32,
            )
            if scale is not None:
                block = block * scale
            out_ref[row, :, :width] = block.astype(out_ref.dtype)
            part += 1


def miss_body(scale, both_ref, other_ref, labels_ref, design_ref, hessian_ref, *out_refs):
    samples = design_ref.shape[0]
    logits = both_ref[:, :samples] + other_ref[:, :samples]
    probability = 1.0 / (1.0 + jnp.exp(-logits))
    hessian_ref[...] = probability * (1.0 - probability)
    miss_rows = (probability - labels_ref[...].astype(jnp.float32)).astype(jnp.bfloat16)
    columns(miss_rows, design_ref, out_refs, scale)


def square_of(residual):
    return jnp.sum(residual * residual, axis=1, keepdims=True)


def gradient_body(summed_ref, weights_ref, lam_ref, sketch_ref, residual_ref, square_ref, payload_ref):
    residual = -(summed_ref[...] + lam_ref[:, :1] * weights_ref[...])
    residual_ref[...] = residual
    lane = lax.broadcasted_iota(jnp.int32, square_ref.shape, 1)
    square_ref[...] = jnp.where(lane == 1, square_of(residual), 0.0)
    repeat(payload_ref, exact_dot(residual, sketch_ref[...], 0).astype(jnp.bfloat16))


def correct(summed_ref, other_ref, lam_ref, values_ref, sketch_ref):
    rank = sketch_ref.shape[1]
    lam = lam_ref[:, :1]
    values = values_ref[...]
    smallest = jnp.min(values, axis=1, keepdims=True)
    ratios = (smallest + lam) / (values + lam) - 1.0
    projected = summed_ref[:, :rank] + other_ref[:, :rank]
    scaled = ratios * projected
    return exact_dot(scaled, sketch_ref[...], 1), jnp.sum(scaled * projected, axis=1, keepdims=True)


def first_body(
    summed_ref, other_ref, lam_ref, values_ref, sketch_ref, residual_ref,
    direction_ref, part_ref, half_ref,
):
    correction, part = correct(summed_ref, other_ref, lam_ref, values_ref, sketch_ref)
    direction = residual_ref[...] + correction
    direction_ref[...] = direction
    part_ref[...] = wide(part)
    half_ref[...] = direction.astype(jnp.bfloat16)


def next_body(
    summed_ref, other_ref, lam_ref, values_ref, sketch_ref, residual_ref, old_ref, old_dot_ref,
    direction_ref, dot_ref, half_ref,
):
    rank = sketch_ref.shape[1]
    correction, part = correct(summed_ref, other_ref, lam_ref, values_ref, sketch_ref)
    res_dot = part + unpack(summed_ref[:, rank:] + other_ref[:, rank:], 0)
    precond_res = residual_ref[...] + correction
    direction = precond_res + (res_dot / old_dot_ref[:, :1]) * old_ref[...]
    direction_ref[...] = direction
    dot_ref[...] = wide(res_dot)
    half_ref[...] = direction.astype(jnp.bfloat16)


def image_of(both_ref, other_ref, hessian_ref, square_ref):
    samples = hessian_ref.shape[1]
    both = both_ref[...] + other_ref[...]
    square_ref[...] = both[:, samples:]
    image_rows = both[:, :samples]
    image = (hessian_ref[...] * image_rows).astype(jnp.bfloat16)
    energy = jnp.sum(image.astype(jnp.float32) * image_rows, axis=1, keepdims=True)
    return image, energy, both[:, samples + 1 : samples + 2]


def image_body(both_ref, other_ref, hessian_ref, design_ref, square_ref, *out_refs):
    image, energy, residual_square = image_of(both_ref, other_ref, hessian_ref, square_ref)
    width = out_refs[0].shape[2] - LANES
    packed = pack(energy, residual_square)
    for out_ref in out_refs:
        for row in range(out_ref.shape[0]):
            out_ref[row, :, width:] = packed.astype(out_ref.dtype)
    columns(image, design_ref, out_refs)


def fold_body(near, *refs):
    own_ref, *received_refs = refs[:near]
    kept_ref, *sent_refs = refs[near:]
    for row in range(own_ref.shape[0]):
        total = own_ref[row]
        for received_ref in received_refs:
            total += received_ref[row].astype(jnp.float32)
        width = total.shape[1] - LANES
        tile = total[:, width:]
        target_ref = ([kept_ref] + sent_refs)[row]
        packed = pack(unpack(tile, 0), unpack(tile, 1))
        target_ref[:, :width] = total[:, :width].astype(target_ref.dtype)
        target_ref[:, width:] = packed.astype(target_ref.dtype)


def step_body(far, *refs):
    kept_ref, *received_refs = refs[:far]
    (
        square_ref, part_ref, lam_ref, direction_ref, residual_ref, update_ref, sketch_ref,
        new_residual_ref, new_update_ref, dot_ref, payload_ref,
    ) = refs[far:]
    width = direction_ref.shape[1]
    rank = sketch_ref.shape[1]
    summed = kept_ref[...]
    for received_ref in received_refs:
        summed += received_ref[...].astype(jnp.float32)
    tile = summed[:, width:]
    lam = lam_ref[:, :1]
    res_dot = part_ref[:, :1] + unpack(tile, 1)
    dot_ref[...] = wide(res_dot)
    step_size = res_dot / (unpack(tile, 0) + lam * square_ref[:, :1])
    direction = direction_ref[...]
    new_update_ref[...] = update_ref[...] + step_size * direction
    residual = residual_ref[...] - step_size * (summed[:, :width] + lam * direction)
    new_residual_ref[...] = residual
    projected = exact_dot(residual, sketch_ref[...], 0).astype(jnp.bfloat16)
    packed = pack(square_of(residual)).astype(jnp.bfloat16)
    for part in range(payload_ref.shape[0]):
        payload_ref[part, :, :rank] = projected
        payload_ref[part, :, rank:] = packed


def energy_body(both_ref, other_ref, hessian_ref, square_ref, payload_ref):
    _, energy, _ = image_of(both_ref, other_ref, hessian_ref, square_ref)
    lane = lax.broadcasted_iota(jnp.int32, (SUBLANES, LANES), 1)
    tile = jnp.zeros((SUBLANES, LANES), jnp.float32)
    for group in range(energy.shape[0] // SUBLANES):
        tile = jnp.where(lane == group, energy[group * SUBLANES : (group + 1) * SUBLANES], tile)
    repeat(payload_ref, tile)


def finish_body(received_ref, square_ref, dot_ref, lam_ref, direction_ref, update_ref, out_ref):
    tile = received_ref[0]
    for part in range(1, received_ref.shape[0]):
        tile += received_ref[part]
    groups = direction_ref.shape[0] // SUBLANES
    energy = jnp.concatenate([tile[:, group : group + 1] for group in range(groups)], axis=0)
    step_size = dot_ref[:, :1] / (energy + lam_ref[:, :1] * square_ref[:, :1])
    out_ref[...] = update_ref[...] + step_size * direction_ref[...]


VMEM = pl.BlockSpec(memory_space=pltpu.VMEM)


def call(body, name, shapes, *operands):
    return pl.pallas_call(
        body,
        out_shape=[jax.ShapeDtypeStruct(shape, dtype) for shape, dtype in shapes],
        in_specs=[VMEM] * len(operands),
        out_specs=[VMEM] * len(shapes),
        compiler_params=pltpu.CompilerParams(vmem_limit_bytes=8 << 20),
        name=name,
    )(*operands)


def load(design, offsets):
    return pl.pallas_call(
        load_body,
        out_shape=pltpu.VMEM(design.shape, design.dtype),
        in_specs=[pl.BlockSpec(memory_space=pltpu.SMEM), pl.BlockSpec(memory_space=pltpu.HBM)],
        out_specs=VMEM,
        scratch_shapes=[pltpu.SemaphoreType.DMA((offsets.shape[0],))],
        compiler_params=pltpu.CompilerParams(vmem_limit_bytes=1 << 20),
        name="load",
    )(offsets, design)


def make_shards(samp, feat):
    near = min(samp, 4)
    far = samp // near

    def swap(values, distance):
        return lax.ppermute(values, "samp", [(i, i ^ distance) for i in range(samp)])

    def far_order():
        return sorted(range(1, far), key=lambda k: (k + 1) % far)

    def swap_far(values_of):
        return {k: swap(values_of(k), near * k) for k in far_order()}

    def gather(block):
        received = swap_far(lambda k: block)
        column = jnp.stack([block] + [received[k] for k in range(1, far)])
        plane = {j: swap(column, j) for j in reversed(range(1, near))}
        return [column] + [plane[j] for j in range(1, near)]

    def exchange(blocks):
        return lax.all_to_all(blocks, "samp", 0, 0)

    def feat_parts(values):
        if feat == 2:
            return values, lax.ppermute(values, "feat", [(0, 1), (1, 0)])
        return lax.psum(values, "feat"), jnp.zeros_like(values)

    def shards(design_matrix, labels, weights, lambdas, sketch, sketch_values):
        strengths, width = weights.shape
        samples = design_matrix.shape[0]
        rank = sketch.shape[1]
        single, half = jnp.float32, jnp.bfloat16
        field = ((strengths, width), single)
        scalars = ((strengths, LANES), single)
        spread = ((strengths, width), half)
        scale = 2.0 ** math.floor(math.log2(HALF_RANGE / (samples * near * LARGEST)))
        lam = jnp.broadcast_to(lambdas[:, None], (strengths, LANES))
        labels = labels[None, :]
        values = sketch_values[None, :]
        mine = lax.axis_index("samp")
        places = jnp.array([k * near + j for j in range(near) for k in range(far)], jnp.int32)
        places = jnp.bitwise_xor(mine, places)
        if width % LANES == 0:
            design = load(design_matrix, places * width)
        else:
            design = design_matrix.reshape(samples, samp, width)
            design = jnp.take(design, places, axis=1).reshape(design_matrix.shape)

        def apply_rows(block, extra):
            shape = ((strengths, samples + LANES), single)
            return feat_parts(call(rows_body, "rows", [shape], *gather(block), design, extra)[0])

        def reduced(blocks):
            return feat_parts(jnp.sum(exchange(blocks).astype(single), axis=0))

        nothing = jnp.zeros((strengths, LANES), single)
        hessian_diag, *outs = call(
            lambda *refs: miss_body(scale, *refs),
            "miss",
            [((strengths, samples), single)] + [((far, strengths, width), single)] * near,
            *apply_rows(weights.astype(half), nothing), labels, design,
        )
        folded = outs[0]
        plane = {j: swap(outs[j].astype(jnp.float16), j) for j in reversed(range(1, near))}
        for j in range(1, near):
            folded = folded + plane[j].astype(single)
        received = swap_far(lambda k: folded[k].astype(jnp.float16))
        summed = folded[0]
        for k in range(1, far):
            summed = summed + received[k].astype(single)
        residual, square, blocks = call(
            gradient_body, "gradient", [field, scalars, ((samp, strengths, rank), half)],
            summed * (1.0 / scale), weights, lam, sketch,
        )
        direction, res_dot, block = call(
            first_body, "first", [field, scalars, spread], *reduced(blocks), lam, values, sketch, residual
        )
        update = weights
        for iteration in range(ITERS):
            parts = apply_rows(block, square)
            if iteration + 1 == ITERS:
                tiny = ((samp, SUBLANES, LANES), single)
                square, blocks = call(energy_body, "energy", [scalars, tiny], *parts, hessian_diag)
                return call(
                    finish_body, "finish", [field],
                    exchange(blocks), square, res_dot, lam, direction, update,
                )[0]
            shape = (far, strengths, width + LANES)
            square, *outs = call(
                image_body, "image", [scalars, (shape, single)] + [(shape, half)] * (near - 1),
                *parts, hessian_diag, design,
            )
            plane = {j: swap(outs[j], j) for j in reversed(range(1, near))}
            kept, *sent = call(
                lambda *refs: fold_body(near, *refs), "fold",
                [(shape[1:], single)] + [(shape[1:], half)] * (far - 1),
                outs[0], *[plane[j] for j in range(1, near)],
            )
            received = swap_far(lambda k: sent[k - 1])
            residual, update, res_dot, blocks = call(
                lambda *refs: step_body(far, *refs), "step",
                [field, field, scalars, ((samp, strengths, rank + LANES), half)],
                kept, *[received[k] for k in range(1, far)],
                square, res_dot, lam, direction, residual, update, sketch,
            )
            direction, res_dot, block = call(
                next_body, "next", [field, scalars, spread],
                *reduced(blocks), lam, values, sketch, residual, direction, res_dot,
            )
            square = nothing

    return shards


def solution(mesh):
    return jax.shard_map(
        make_shards(mesh.shape["samp"], mesh.shape["feat"]),
        mesh=mesh,
        in_specs=(
            P("samp", "feat"),
            P("samp"),
            P(None, ("feat", "samp")),
            P(),
            P(("feat", "samp"), None),
            P(),
        ),
        out_specs=P(None, ("feat", "samp")),
        check_vma=False,
    )
```

time: 155 us -> 139 us (0.90)
  blocking collectives: 138 us -> 38.2 us
  starting transfers between devices: 0.15 us -> 41.4 us
  waiting for transfers between devices: 5.98 us -> 45.6 us
  other arithmetic: 0.25 us -> 2.64 us
    all_to_all x8 -> x3, blocking collectives: 138 us -> 38.2 us  [exchange(): return lax.all_to_all(blocks, 'samp', 0, 0)]
    ppermute x0 -> x30, starting transfers between devices: none -> 41.2 us  [swap(): lax.ppermute(values, 'samp', [(i, i ^ distance) for i in range(samp)])]
    ppermute x0 -> x30, waiting for transfers between devices: none -> 39.6 us  [swap(): lax.ppermute(values, 'samp', [(i, i ^ distance) for i in range(samp)])]
  transfers between devices with their start and end apart: 5 -> 35, of which waited for: 5 -> 25; matrix products, arithmetic and copies ran while one was open for 0% -> 1% of each run, Pallas kernels for 0% -> 1%
where the time goes in v3:
time: 139 us
  waiting for transfers between devices  45.6 us (33%)
  starting transfers between devices  41.4 us (30%)
  blocking collectives  38.2 us (27%)
  Pallas kernels  8.59 us (6%)
  other arithmetic  2.64 us (2%)
  local copies, waits for them, and re-layouts  2.3 us (2%)
    ppermute x30, starting transfers between devices, swap(): lax.ppermute(values, 'samp', [(i, i ^ distance) for i in range(samp)])  41.2 us
    ppermute x30, waiting for transfers between devices, swap(): lax.ppermute(values, 'samp', [(i, i ^ distance) for i in range(samp)])  39.6 us
    all_to_all x3, blocking collectives, exchange(): return lax.all_to_all(blocks, 'samp', 0, 0)  38.2 us
    pallas_call x12, Pallas kernels, call(): pl.pallas_call(body, out_shape=[jax.ShapeDtypeStruct(shape, dtype) for sh...  7.56 us
    ppermute x5, waiting for transfers between devices, feat_parts(): return (values, lax.ppermute(values, 'feat', [(0, 1), (1, 0)]))  5.93 us
  transfers between devices with their start and end apart: 35, of which 25 were waited for; matrix products, arithmetic and copies ran while one was open for 1% of the time, Pallas kernels for 1%

profile of v3, /device:TPU:0, one launch (start us, length us, event | category | flops | bytes accessed | tf_op | source)
XLA Modules:
  0.0 138.9 jit_solution(6824970620398020592)
XLA Ops:
  0.8 3.1 %collective-permute-start = (bf16[16,1024]{1,0:T(8,128)(2,1)S(1)}, bf16[16,1024]{1,0:T(8,128)(2,1)S(1)}, u32[]{:S(2)}, u32[]{:S(2)}) collective-permute-start(bf16[16,1024]{1,0:T(8,128)(2,1)S(1)} %convert_element_type.48), channel_id=1, source_target_pairs={{0,8},{2,10},{4,12},{6,14},{8,0},{10,2},{12,4},{14,6},{16,24},{18,... | collective-permute-start | bytes 98312 | tf_op jit(solution)/shard_map/ppermute | solution.py:290
  3.9 2.6 %collective-permute-start.1 = (bf16[16,1024]{1,0:T(8,128)(2,1)S(1)}, bf16[16,1024]{1,0:T(8,128)(2,1)S(1)}, u32[]{:S(2)}, u32[]{:S(2)}) collective-permute-start(bf16[16,1024]{1,0:T(8,128)(2,1)S(1)} %convert_element_type.48), channel_id=1, source_target_pairs={{0,16},{2,18},{4,20},{6,22},{8,24},{10,26},{12,28},{14,30},{16,0},... | collective-permute-start | bytes 98312 | tf_op jit(solution)/shard_map/ppermute | solution.py:290
  7.3 2.0 %collective-permute-done.1 = bf16[16,1024]{1,0:T(8,128)(2,1)S(1)} collective-permute-done((bf16[16,1024]{1,0:T(8,128)(2,1)S(1)}, bf16[16,1024]{1,0:T(8,128)(2,1)S(1)}, u32[]{:S(2)}, u32[]{:S(2)}) %collective-permute-start.1) | collective-permute-done | bytes 32800 | tf_op jit(solution)/shard_map/ppermute | solution.py:290
  9.3 2.9 %collective-permute-done.2 = bf16[16,1024]{1,0:T(8,128)(2,1)S(1)} collective-permute-done((bf16[16,1024]{1,0:T(8,128)(2,1)S(1)}, bf16[16,1024]{1,0:T(8,128)(2,1)S(1)}, u32[]{:S(2)}, u32[]{:S(2)}) %collective-permute-start.2) | collective-permute-done | bytes 32800 | tf_op jit(solution)/shard_map/ppermute | solution.py:290
  12.2 1.6 %collective-permute-start.3 = (bf16[4,16,1024]{2,1,0:T(8,128)(2,1)S(1)}, bf16[4,16,1024]{2,1,0:T(8,128)(2,1)S(1)}, u32[]{:S(2)}, u32[]{:S(2)}) collective-permute-start(bf16[4,16,1024]{2,1,0:T(8,128)(2,1)S(1)} %pad_maximum_fusion.refs_0_), channel_id=1, source_target_pairs={{0,2},{2,0},{4,6},{6,4},{8,10},{10,8},{12,14},{14,12},{16,18},{18,... | collective-permute-start | bytes 393224 | tf_op jit(solution)/shard_map/ppermute | solution.py:290
  13.8 1.5 %collective-permute-start.4 = (bf16[4,16,1024]{2,1,0:T(8,128)(2,1)S(1)}, bf16[4,16,1024]{2,1,0:T(8,128)(2,1)S(1)}, u32[]{:S(2)}, u32[]{:S(2)}) collective-permute-start(bf16[4,16,1024]{2,1,0:T(8,128)(2,1)S(1)} %pad_maximum_fusion.refs_0_), channel_id=1, source_target_pairs={{0,4},{2,6},{4,0},{6,2},{8,12},{10,14},{12,8},{14,10},{16,20},{18,... | collective-permute-start | bytes 393224 | tf_op jit(solution)/shard_map/ppermute | solution.py:290
  16.4 2.2 %copy-done.1 = bf16[128,16384]{1,0:T(8,128)(2,1)S(1)} copy-done((bf16[128,16384]{1,0:T(8,128)(2,1)S(1)}, bf16[128,16384]{1,0:T(8,128)(2,1)}, u32[]{:S(2)}) %copy-start.1) | copy-done | bytes 4194328
  18.6 1.0 load.1.refs_4_.refs_3_.design_ref
  19.7 1.5 %collective-permute-done.5.refs_3_ = bf16[4,16,1024]{2,1,0:T(8,128)(2,1)S(1)} collective-permute-done((bf16[4,16,1024]{2,1,0:T(8,128)(2,1)S(1)}, bf16[4,16,1024]{2,1,0:T(8,128)(2,1)S(1)}, u32[]{:S(2)}, u32[]{:S(2)}) %collective-permute-start.5) | collective-permute-done | bytes 131104 | tf_op jit(solution)/shard_map/ppermute | solution.py:290
  21.2 1.2 rows.3.refs_0_
  22.5 1.2 collective-permute-done.6.refs_1_
  24.9 1.1 collective-permute-start.8
  26.1 2.0 %collective-permute-start.9 = (f16[4,16,1024]{2,1,0:T(8,128)(2,1)S(1)}, f16[4,16,1024]{2,1,0:T(8,128)(2,1)S(1)}, u32[]{:S(2)}, u32[]{:S(2)}) collective-permute-start(f16[4,16,1024]{2,1,0:T(8,128)(2,1)S(1)} %convert_element_type.53), channel_id=1, source_target_pairs={{0,6},{2,4},{4,2},{6,0},{8,14},{10,12},{12,10},{14,8},{16,22},{18,... | collective-permute-start | bytes 393224 | tf_op jit(solution)/shard_map/ppermute | solution.py:290
  28.0 2.7 %collective-permute-done.7 = f16[4,16,1024]{2,1,0:T(8,128)(2,1)S(1)} collective-permute-done((f16[4,16,1024]{2,1,0:T(8,128)(2,1)S(1)}, f16[4,16,1024]{2,1,0:T(8,128)(2,1)S(1)}, u32[]{:S(2)}, u32[]{:S(2)}) %collective-permute-start.7) | collective-permute-done | bytes 131104 | tf_op jit(solution)/shard_map/ppermute | solution.py:290
  30.8 2.3 %collective-permute-done.8 = f16[4,16,1024]{2,1,0:T(8,128)(2,1)S(1)} collective-permute-done((f16[4,16,1024]{2,1,0:T(8,128)(2,1)S(1)}, f16[4,16,1024]{2,1,0:T(8,128)(2,1)S(1)}, u32[]{:S(2)}, u32[]{:S(2)}) %collective-permute-start.8) | collective-permute-done | bytes 131104 | tf_op jit(solution)/shard_map/ppermute | solution.py:290
  33.3 1.0 collective-permute-start.11
  34.3 3.4 %collective-permute-start.12 = (f16[16,1024]{1,0:T(8,128)(2,1)S(1)}, f16[16,1024]{1,0:T(8,128)(2,1)S(1)}, u32[]{:S(2)}, u32[]{:S(2)}) collective-permute-start(f16[16,1024]{1,0:T(8,128)(2,1)S(1)} %get-tuple-element.66), channel_id=1, source_target_pairs={{0,24},{2,26},{4,28},{6,30},{8,16},{10,18},{12,20},{14,22},{16,8},... | collective-permute-start | bytes 98312 | tf_op jit(solution)/shard_map/ppermute | solution.py:290
  38.3 1.8 %collective-permute-done.12 = f16[16,1024]{1,0:T(8,128)(2,1)S(1)} collective-permute-done((f16[16,1024]{1,0:T(8,128)(2,1)S(1)}, f16[16,1024]{1,0:T(8,128)(2,1)S(1)}, u32[]{:S(2)}, u32[]{:S(2)}) %collective-permute-start.12) | collective-permute-done | bytes 32800 | tf_op jit(solution)/shard_map/ppermute | solution.py:290
  40.4 13.8 %all_to_all.15 = bf16[16,16,384]{2,1,0:T(8,128)(2,1)S(1)} all-to-all(bf16[16,16,384]{2,1,0:T(8,128)(2,1)S(1)} %get-tuple-element.38), channel_id=1, replica_groups=mesh['samp'=16,'feat'=2] {'samp'}, dimensions={0} | all-to-all | bytes 393216 | tf_op jit(solution)/shard_map/all_to_all | solution.py:305
  54.4 1.2 collective-permute-done.13.other_ref
  56.8 1.3 collective-permute-start.15
  58.1 2.2 %collective-permute-start.16 = (bf16[16,1024]{1,0:T(8,128)(2,1)S(1)}, bf16[16,1024]{1,0:T(8,128)(2,1)S(1)}, u32[]{:S(2)}, u32[]{:S(2)}) collective-permute-start(bf16[16,1024]{1,0:T(8,128)(2,1)S(1)} %get-tuple-element.40), channel_id=1, source_target_pairs={{0,24},{2,26},{4,28},{6,30},{8,16},{10,18},{12,20},{14,22},{16,8},... | collective-permute-start | bytes 98312 | tf_op jit(solution)/shard_map/ppermute | solution.py:290
  60.4 1.4 %collective-permute-done.15 = bf16[16,1024]{1,0:T(8,128)(2,1)S(1)} collective-permute-done((bf16[16,1024]{1,0:T(8,128)(2,1)S(1)}, bf16[16,1024]{1,0:T(8,128)(2,1)S(1)}, u32[]{:S(2)}, u32[]{:S(2)}) %collective-permute-start.15) | collective-permute-done | bytes 32800 | tf_op jit(solution)/shard_map/ppermute | solution.py:290
  61.8 2.1 %collective-permute-done.16 = bf16[16,1024]{1,0:T(8,128)(2,1)S(1)} collective-permute-done((bf16[16,1024]{1,0:T(8,128)(2,1)S(1)}, bf16[16,1024]{1,0:T(8,128)(2,1)S(1)}, u32[]{:S(2)}, u32[]{:S(2)}) %collective-permute-start.16) | collective-permute-done | bytes 32800 | tf_op jit(solution)/shard_map/ppermute | solution.py:290
  65.2 2.2 %collective-permute-start.19 = (bf16[4,16,1024]{2,1,0:T(8,128)(2,1)S(1)}, bf16[4,16,1024]{2,1,0:T(8,128)(2,1)S(1)}, u32[]{:S(2)}, u32[]{:S(2)}) collective-permute-start(bf16[4,16,1024]{2,1,0:T(8,128)(2,1)S(1)} %pad_maximum_fusion.1.refs_0_), channel_id=1, source_target_pairs={{0,6},{2,4},{4,2},{6,0},{8,14},{10,12},{12,10},{14,8},{16,22},{18,... | collective-permute-start | bytes 393224 | tf_op jit(solution)/shard_map/ppermute | solution.py:290
  67.4 2.0 %collective-permute-done.17.refs_1_ = bf16[4,16,1024]{2,1,0:T(8,128)(2,1)S(1)} collective-permute-done((bf16[4,16,1024]{2,1,0:T(8,128)(2,1)S(1)}, bf16[4,16,1024]{2,1,0:T(8,128)(2,1)S(1)}, u32[]{:S(2)}, u32[]{:S(2)}) %collective-permute-start.17) | collective-permute-done | bytes 131104 | tf_op jit(solution)/shard_map/ppermute | solution.py:290
  69.4 1.9 %collective-permute-done.18.refs_2_ = bf16[4,16,1024]{2,1,0:T(8,128)(2,1)S(1)} collective-permute-done((bf16[4,16,1024]{2,1,0:T(8,128)(2,1)S(1)}, bf16[4,16,1024]{2,1,0:T(8,128)(2,1)S(1)}, u32[]{:S(2)}, u32[]{:S(2)}) %collective-permute-start.18) | collective-permute-done | bytes 131104 | tf_op jit(solution)/shard_map/ppermute | solution.py:290
  71.2 1.2 rows.4.both_ref
  72.4 1.2 collective-permute-done.20.other_ref
  74.3 1.9 %collective-permute-start.21 = (bf16[4,16,1152]{2,1,0:T(8,128)(2,1)S(1)}, bf16[4,16,1152]{2,1,0:T(8,128)(2,1)S(1)}, u32[]{:S(2)}, u32[]{:S(2)}) collective-permute-start(bf16[4,16,1152]{2,1,0:T(8,128)(2,1)S(1)} %get-tuple-element.44), channel_id=1, source_target_pairs={{0,2},{2,0},{4,6},{6,4},{8,10},{10,8},{12,14},{14,12},{16,18},{18,... | collective-permute-start | bytes 442376 | tf_op jit(solution)/shard_map/ppermute | solution.py:290
  76.2 1.0 collective-permute-start.22
  77.8 3.1 %collective-permute-done.21.refs_1_ = bf16[4,16,1152]{2,1,0:T(8,128)(2,1)S(1)} collective-permute-done((bf16[4,16,1152]{2,1,0:T(8,128)(2,1)S(1)}, bf16[4,16,1152]{2,1,0:T(8,128)(2,1)S(1)}, u32[]{:S(2)}, u32[]{:S(2)}) %collective-permute-start.21) | collective-permute-done | bytes 147488 | tf_op jit(solution)/shard_map/ppermute | solution.py:290
  80.9 4.1 %collective-permute-done.22.refs_2_ = bf16[4,16,1152]{2,1,0:T(8,128)(2,1)S(1)} collective-permute-done((bf16[4,16,1152]{2,1,0:T(8,128)(2,1)S(1)}, bf16[4,16,1152]{2,1,0:T(8,128)(2,1)S(1)}, u32[]{:S(2)}, u32[]{:S(2)}) %collective-permute-start.22) | collective-permute-done | bytes 147488 | tf_op jit(solution)/shard_map/ppermute | solution.py:290
  85.3 2.6 %collective-permute-start.25 = (bf16[16,1152]{1,0:T(8,128)(2,1)S(1)}, bf16[16,1152]{1,0:T(8,128)(2,1)S(1)}, u32[]{:S(2)}, u32[]{:S(2)}) collective-permute-start(bf16[16,1152]{1,0:T(8,128)(2,1)S(1)} %get-tuple-element.49), channel_id=1, source_target_pairs={{0,16},{2,18},{4,20},{6,22},{8,24},{10,26},{12,28},{14,30},{16,0},... | collective-permute-start | bytes 110600 | tf_op jit(solution)/shard_map/ppermute | solution.py:290
  87.9 1.8 %collective-permute-start.26 = (bf16[16,1152]{1,0:T(8,128)(2,1)S(1)}, bf16[16,1152]{1,0:T(8,128)(2,1)S(1)}, u32[]{:S(2)}, u32[]{:S(2)}) collective-permute-start(bf16[16,1152]{1,0:T(8,128)(2,1)S(1)} %get-tuple-element.50), channel_id=1, source_target_pairs={{0,24},{2,26},{4,28},{6,30},{8,16},{10,18},{12,20},{14,22},{16,8},... | collective-permute-start | bytes 110600 | tf_op jit(solution)/shard_map/ppermute | solution.py:290
  90.2 3.5 %collective-permute-done.26.refs_3_ = bf16[16,1152]{1,0:T(8,128)(2,1)S(1)} collective-permute-done((bf16[16,1152]{1,0:T(8,128)(2,1)S(1)}, bf16[16,1152]{1,0:T(8,128)(2,1)S(1)}, u32[]{:S(2)}, u32[]{:S(2)}) %collective-permute-start.26) | collective-permute-done | bytes 36896 | tf_op jit(solution)/shard_map/ppermute | solution.py:290
  94.1 12.1 %all_to_all.16 = bf16[16,16,512]{2,1,0:T(8,128)(2,1)S(1)} all-to-all(bf16[16,16,512]{2,1,0:T(8,128)(2,1)S(1)} %get-tuple-element.54), channel_id=1, replica_groups=mesh['samp'=16,'feat'=2] {'samp'}, dimensions={0} | all-to-all | bytes 524288 | tf_op jit(solution)/shard_map/all_to_all | solution.py:305
  106.3 1.2 collective-permute-done.27.other_ref
  108.7 1.6 %collective-permute-start.29 = (bf16[16,1024]{1,0:T(8,128)(2,1)S(1)}, bf16[16,1024]{1,0:T(8,128)(2,1)S(1)}, u32[]{:S(2)}, u32[]{:S(2)}) collective-permute-start(bf16[16,1024]{1,0:T(8,128)(2,1)S(1)} %get-tuple-element.57), channel_id=1, source_target_pairs={{0,16},{2,18},{4,20},{6,22},{8,24},{10,26},{12,28},{14,30},{16,0},... | collective-permute-start | bytes 98312 | tf_op jit(solution)/shard_map/ppermute | solution.py:290
  110.3 2.0 %collective-permute-start.30 = (bf16[16,1024]{1,0:T(8,128)(2,1)S(1)}, bf16[16,1024]{1,0:T(8,128)(2,1)S(1)}, u32[]{:S(2)}, u32[]{:S(2)}) collective-permute-start(bf16[16,1024]{1,0:T(8,128)(2,1)S(1)} %get-tuple-element.57), channel_id=1, source_target_pairs={{0,24},{2,26},{4,28},{6,30},{8,16},{10,18},{12,20},{14,22},{16,8},... | collective-permute-start | bytes 98312 | tf_op jit(solution)/shard_map/ppermute | solution.py:290
  112.3 1.4 %collective-permute-done.29 = bf16[16,1024]{1,0:T(8,128)(2,1)S(1)} collective-permute-done((bf16[16,1024]{1,0:T(8,128)(2,1)S(1)}, bf16[16,1024]{1,0:T(8,128)(2,1)S(1)}, u32[]{:S(2)}, u32[]{:S(2)}) %collective-permute-start.29) | collective-permute-done | bytes 32800 | tf_op jit(solution)/shard_map/ppermute | solution.py:290
  113.7 2.3 %collective-permute-done.30 = bf16[16,1024]{1,0:T(8,128)(2,1)S(1)} collective-permute-done((bf16[16,1024]{1,0:T(8,128)(2,1)S(1)}, bf16[16,1024]{1,0:T(8,128)(2,1)S(1)}, u32[]{:S(2)}, u32[]{:S(2)}) %collective-permute-start.30) | collective-permute-done | bytes 32800 | tf_op jit(solution)/shard_map/ppermute | solution.py:290
  117.4 2.2 %collective-permute-start.33 = (bf16[4,16,1024]{2,1,0:T(8,128)(2,1)S(1)}, bf16[4,16,1024]{2,1,0:T(8,128)(2,1)S(1)}, u32[]{:S(2)}, u32[]{:S(2)}) collective-permute-start(bf16[4,16,1024]{2,1,0:T(8,128)(2,1)S(1)} %pad_maximum_fusion.2.refs_0_), channel_id=1, source_target_pairs={{0,6},{2,4},{4,2},{6,0},{8,14},{10,12},{12,10},{14,8},{16,22},{18,... | collective-permute-start | bytes 393224 | tf_op jit(solution)/shard_map/ppermute | solution.py:290
  119.6 1.8 %collective-permute-done.31.refs_1_ = bf16[4,16,1024]{2,1,0:T(8,128)(2,1)S(1)} collective-permute-done((bf16[4,16,1024]{2,1,0:T(8,128)(2,1)S(1)}, bf16[4,16,1024]{2,1,0:T(8,128)(2,1)S(1)}, u32[]{:S(2)}, u32[]{:S(2)}) %collective-permute-start.31) | collective-permute-done | bytes 131104 | tf_op jit(solution)/shard_map/ppermute | solution.py:290
  121.9 1.4 %collective-permute-done.33.refs_3_ = bf16[4,16,1024]{2,1,0:T(8,128)(2,1)S(1)} collective-permute-done((bf16[4,16,1024]{2,1,0:T(8,128)(2,1)S(1)}, bf16[4,16,1024]{2,1,0:T(8,128)(2,1)S(1)}, u32[]{:S(2)}, u32[]{:S(2)}) %collective-permute-start.33) | collective-permute-done | bytes 131104 | tf_op jit(solution)/shard_map/ppermute | solution.py:290
  123.3 1.2 rows.5.both_ref
  124.5 1.2 collective-permute-done.34.other_ref
  125.8 12.3 %all_to_all.17.received_ref = f32[16,8,128]{2,1,0:T(8,128)S(1)} all-to-all(f32[16,8,128]{2,1,0:T(8,128)S(1)} %get-tuple-element.58), channel_id=1, replica_groups=mesh['samp'=16,'feat'=2] {'samp'}, dimensions={0} | all-to-all | bytes 131072 | tf_op jit(solution)/shard_map/all_to_all | solution.py:305
  (67 shorter events, 14.7 us)
Async XLA Ops:
  0.8 6.5 %collective-permute-start = (bf16[16,1024]{1,0:T(8,128)(2,1)S(1)}, bf16[16,1024]{1,0:T(8,128)(2,1)S(1)}, u32[]{:S(2)}, u32[]{:S(2)}) collective-permute-start(bf16[16,1024]{1,0:T(8,128)(2,1)S(1)} %convert_element_type.48), channel_id=1, source_target_pairs={{0,8},{2,10},{4,12},{6,14},{8,0},{10,2},{12,4},{14,6},{16,24},{18,... | collective-permute-start | bytes 98312 | tf_op jit(solution)/shard_map/ppermute | solution.py:290
  3.9 5.4 %collective-permute-start.1 = (bf16[16,1024]{1,0:T(8,128)(2,1)S(1)}, bf16[16,1024]{1,0:T(8,128)(2,1)S(1)}, u32[]{:S(2)}, u32[]{:S(2)}) collective-permute-start(bf16[16,1024]{1,0:T(8,128)(2,1)S(1)} %convert_element_type.48), channel_id=1, source_target_pairs={{0,16},{2,18},{4,20},{6,22},{8,24},{10,26},{12,28},{14,30},{16,0},... | collective-permute-start | bytes 98312 | tf_op jit(solution)/shard_map/ppermute | solution.py:290
  6.5 5.7 %collective-permute-start.2 = (bf16[16,1024]{1,0:T(8,128)(2,1)S(1)}, bf16[16,1024]{1,0:T(8,128)(2,1)S(1)}, u32[]{:S(2)}, u32[]{:S(2)}) collective-permute-start(bf16[16,1024]{1,0:T(8,128)(2,1)S(1)} %convert_element_type.48), channel_id=1, source_target_pairs={{0,24},{2,26},{4,28},{6,30},{8,16},{10,18},{12,20},{14,22},{16,8},... | collective-permute-start | bytes 98312 | tf_op jit(solution)/shard_map/ppermute | solution.py:290
  12.2 7.5 %collective-permute-start.3 = (bf16[4,16,1024]{2,1,0:T(8,128)(2,1)S(1)}, bf16[4,16,1024]{2,1,0:T(8,128)(2,1)S(1)}, u32[]{:S(2)}, u32[]{:S(2)}) collective-permute-start(bf16[4,16,1024]{2,1,0:T(8,128)(2,1)S(1)} %pad_maximum_fusion.refs_0_), channel_id=1, source_target_pairs={{0,2},{2,0},{4,6},{6,4},{8,10},{10,8},{12,14},{14,12},{16,18},{18,... | collective-permute-start | bytes 393224 | tf_op jit(solution)/shard_map/ppermute | solution.py:290
  13.8 5.9 %collective-permute-start.4 = (bf16[4,16,1024]{2,1,0:T(8,128)(2,1)S(1)}, bf16[4,16,1024]{2,1,0:T(8,128)(2,1)S(1)}, u32[]{:S(2)}, u32[]{:S(2)}) collective-permute-start(bf16[4,16,1024]{2,1,0:T(8,128)(2,1)S(1)} %pad_maximum_fusion.refs_0_), channel_id=1, source_target_pairs={{0,4},{2,6},{4,0},{6,2},{8,12},{10,14},{12,8},{14,10},{16,20},{18,... | collective-permute-start | bytes 393224 | tf_op jit(solution)/shard_map/ppermute | solution.py:290
  15.3 5.9 %collective-permute-start.5 = (bf16[4,16,1024]{2,1,0:T(8,128)(2,1)S(1)}, bf16[4,16,1024]{2,1,0:T(8,128)(2,1)S(1)}, u32[]{:S(2)}, u32[]{:S(2)}) collective-permute-start(bf16[4,16,1024]{2,1,0:T(8,128)(2,1)S(1)} %pad_maximum_fusion.refs_0_), channel_id=1, source_target_pairs={{0,6},{2,4},{4,2},{6,0},{8,14},{10,12},{12,10},{14,8},{16,22},{18,... | collective-permute-start | bytes 393224 | tf_op jit(solution)/shard_map/ppermute | solution.py:290
  16.4 2.2 %copy-start.1 = (bf16[128,16384]{1,0:T(8,128)(2,1)S(1)}, bf16[128,16384]{1,0:T(8,128)(2,1)}, u32[]{:S(2)}) copy-start(bf16[128,16384]{1,0:T(8,128)(2,1)} %design_ref.1) | copy-start | bytes 12582916
  19.7 4.0 %copy-start.3 = (s32[128]{0:T(128)S(1)}, s32[128]{0:T(128)}, u32[]{:S(2)}) copy-start(s32[128]{0:T(128)} %param.8) | copy-start | bytes 1540
  22.4 17.7 %copy-start.5 = (f32[16]{0:T(128)S(1)}, f32[16]{0:T(128)}, u32[]{:S(2)}) copy-start(f32[16]{0:T(128)} %param.10) | copy-start | bytes 196
  22.4 17.8 %copy-start = (bf16[1024,384]{1,0:T(8,128)(2,1)S(1)}, bf16[1024,384]{1,0:T(8,128)(2,1)}, u32[]{:S(2)}) copy-start(bf16[1024,384]{1,0:T(8,128)(2,1)} %sketch_ref.5) | copy-start | bytes 2359300
  22.4 17.8 %copy-start.2 = (f32[16,1024]{1,0:T(8,128)S(1)}, f32[16,1024]{1,0:T(8,128)}, u32[]{:S(2)}) copy-start(f32[16,1024]{1,0:T(8,128)} %refs_9_.1) | copy-start | bytes 196612
  22.4 1.2 collective-permute-start.6
  23.6 30.7 %copy-start.4 = (f32[384]{0:T(512)S(1)}, f32[384]{0:T(512)}, u32[]{:S(2)}) copy-start(f32[384]{0:T(512)} %param.12) | copy-start | bytes 4612
  24.3 6.4 %collective-permute-start.7 = (f16[4,16,1024]{2,1,0:T(8,128)(2,1)S(1)}, f16[4,16,1024]{2,1,0:T(8,128)(2,1)S(1)}, u32[]{:S(2)}, u32[]{:S(2)}) collective-permute-start(f16[4,16,1024]{2,1,0:T(8,128)(2,1)S(1)} %convert_element_type.49), channel_id=1, source_target_pairs={{0,2},{2,0},{4,6},{6,4},{8,10},{10,8},{12,14},{14,12},{16,18},{18,... | collective-permute-start | bytes 393224 | tf_op jit(solution)/shard_map/ppermute | solution.py:290
  24.9 8.2 %collective-permute-start.8 = (f16[4,16,1024]{2,1,0:T(8,128)(2,1)S(1)}, f16[4,16,1024]{2,1,0:T(8,128)(2,1)S(1)}, u32[]{:S(2)}, u32[]{:S(2)}) collective-permute-start(f16[4,16,1024]{2,1,0:T(8,128)(2,1)S(1)} %convert_element_type.51), channel_id=1, source_target_pairs={{0,4},{2,6},{4,0},{6,2},{8,12},{10,14},{12,8},{14,10},{16,20},{18,... | collective-permute-start | bytes 393224 | tf_op jit(solution)/shard_map/ppermute | solution.py:290
  26.1 7.1 %collective-permute-start.9 = (f16[4,16,1024]{2,1,0:T(8,128)(2,1)S(1)}, f16[4,16,1024]{2,1,0:T(8,128)(2,1)S(1)}, u32[]{:S(2)}, u32[]{:S(2)}) collective-permute-start(f16[4,16,1024]{2,1,0:T(8,128)(2,1)S(1)} %convert_element_type.53), channel_id=1, source_target_pairs={{0,6},{2,4},{4,2},{6,0},{8,14},{10,12},{12,10},{14,8},{16,22},{18,... | collective-permute-start | bytes 393224 | tf_op jit(solution)/shard_map/ppermute | solution.py:290
  33.2 4.5 %collective-permute-start.10 = (f16[16,1024]{1,0:T(8,128)(2,1)S(1)}, f16[16,1024]{1,0:T(8,128)(2,1)S(1)}, u32[]{:S(2)}, u32[]{:S(2)}) collective-permute-start(f16[16,1024]{1,0:T(8,128)(2,1)S(1)} %get-tuple-element.65), channel_id=1, source_target_pairs={{0,8},{2,10},{4,12},{6,14},{8,0},{10,2},{12,4},{14,6},{16,24},{18,... | collective-permute-start | bytes 98312 | tf_op jit(solution)/shard_map/ppermute | solution.py:290
  33.3 5.0 %collective-permute-start.11 = (f16[16,1024]{1,0:T(8,128)(2,1)S(1)}, f16[16,1024]{1,0:T(8,128)(2,1)S(1)}, u32[]{:S(2)}, u32[]{:S(2)}) collective-permute-start(f16[16,1024]{1,0:T(8,128)(2,1)S(1)} %get-tuple-element.67), channel_id=1, source_target_pairs={{0,16},{2,18},{4,20},{6,22},{8,24},{10,26},{12,28},{14,30},{16,0},... | collective-permute-start | bytes 98312 | tf_op jit(solution)/shard_map/ppermute | solution.py:290
  34.3 5.7 %collective-permute-start.12 = (f16[16,1024]{1,0:T(8,128)(2,1)S(1)}, f16[16,1024]{1,0:T(8,128)(2,1)S(1)}, u32[]{:S(2)}, u32[]{:S(2)}) collective-permute-start(f16[16,1024]{1,0:T(8,128)(2,1)S(1)} %get-tuple-element.66), channel_id=1, source_target_pairs={{0,24},{2,26},{4,28},{6,30},{8,16},{10,18},{12,20},{14,22},{16,8},... | collective-permute-start | bytes 98312 | tf_op jit(solution)/shard_map/ppermute | solution.py:290
  54.3 1.3 collective-permute-start.13
  55.9 4.4 %collective-permute-start.14 = (bf16[16,1024]{1,0:T(8,128)(2,1)S(1)}, bf16[16,1024]{1,0:T(8,128)(2,1)S(1)}, u32[]{:S(2)}, u32[]{:S(2)}) collective-permute-start(bf16[16,1024]{1,0:T(8,128)(2,1)S(1)} %get-tuple-element.40), channel_id=1, source_target_pairs={{0,8},{2,10},{4,12},{6,14},{8,0},{10,2},{12,4},{14,6},{16,24},{18,... | collective-permute-start | bytes 98312 | tf_op jit(solution)/shard_map/ppermute | solution.py:290
  56.8 5.0 %collective-permute-start.15 = (bf16[16,1024]{1,0:T(8,128)(2,1)S(1)}, bf16[16,1024]{1,0:T(8,128)(2,1)S(1)}, u32[]{:S(2)}, u32[]{:S(2)}) collective-permute-start(bf16[16,1024]{1,0:T(8,128)(2,1)S(1)} %get-tuple-element.40), channel_id=1, source_target_pairs={{0,16},{2,18},{4,20},{6,22},{8,24},{10,26},{12,28},{14,30},{16,0},... | collective-permute-start | bytes 98312 | tf_op jit(solution)/shard_map/ppermute | solution.py:290
  58.1 5.7 %collective-permute-start.16 = (bf16[16,1024]{1,0:T(8,128)(2,1)S(1)}, bf16[16,1024]{1,0:T(8,128)(2,1)S(1)}, u32[]{:S(2)}, u32[]{:S(2)}) collective-permute-start(bf16[16,1024]{1,0:T(8,128)(2,1)S(1)} %get-tuple-element.40), channel_id=1, source_target_pairs={{0,24},{2,26},{4,28},{6,30},{8,16},{10,18},{12,20},{14,22},{16,8},... | collective-permute-start | bytes 98312 | tf_op jit(solution)/shard_map/ppermute | solution.py:290
  63.9 5.5 %collective-permute-start.17 = (bf16[4,16,1024]{2,1,0:T(8,128)(2,1)S(1)}, bf16[4,16,1024]{2,1,0:T(8,128)(2,1)S(1)}, u32[]{:S(2)}, u32[]{:S(2)}) collective-permute-start(bf16[4,16,1024]{2,1,0:T(8,128)(2,1)S(1)} %pad_maximum_fusion.1.refs_0_), channel_id=1, source_target_pairs={{0,2},{2,0},{4,6},{6,4},{8,10},{10,8},{12,14},{14,12},{16,18},{18,... | collective-permute-start | bytes 393224 | tf_op jit(solution)/shard_map/ppermute | solution.py:290
  64.5 6.7 %collective-permute-start.18 = (bf16[4,16,1024]{2,1,0:T(8,128)(2,1)S(1)}, bf16[4,16,1024]{2,1,0:T(8,128)(2,1)S(1)}, u32[]{:S(2)}, u32[]{:S(2)}) collective-permute-start(bf16[4,16,1024]{2,1,0:T(8,128)(2,1)S(1)} %pad_maximum_fusion.1.refs_0_), channel_id=1, source_target_pairs={{0,4},{2,6},{4,0},{6,2},{8,12},{10,14},{12,8},{14,10},{16,20},{18,... | collective-permute-start | bytes 393224 | tf_op jit(solution)/shard_map/ppermute | solution.py:290
  65.2 6.0 %collective-permute-start.19 = (bf16[4,16,1024]{2,1,0:T(8,128)(2,1)S(1)}, bf16[4,16,1024]{2,1,0:T(8,128)(2,1)S(1)}, u32[]{:S(2)}, u32[]{:S(2)}) collective-permute-start(bf16[4,16,1024]{2,1,0:T(8,128)(2,1)S(1)} %pad_maximum_fusion.1.refs_0_), channel_id=1, source_target_pairs={{0,6},{2,4},{4,2},{6,0},{8,14},{10,12},{12,10},{14,8},{16,22},{18,... | collective-permute-start | bytes 393224 | tf_op jit(solution)/shard_map/ppermute | solution.py:290
  72.4 1.2 collective-permute-start.20
  74.3 6.6 %collective-permute-start.21 = (bf16[4,16,1152]{2,1,0:T(8,128)(2,1)S(1)}, bf16[4,16,1152]{2,1,0:T(8,128)(2,1)S(1)}, u32[]{:S(2)}, u32[]{:S(2)}) collective-permute-start(bf16[4,16,1152]{2,1,0:T(8,128)(2,1)S(1)} %get-tuple-element.44), channel_id=1, source_target_pairs={{0,2},{2,0},{4,6},{6,4},{8,10},{10,8},{12,14},{14,12},{16,18},{18,... | collective-permute-start | bytes 442376 | tf_op jit(solution)/shard_map/ppermute | solution.py:290
  76.2 8.8 %collective-permute-start.22 = (bf16[4,16,1152]{2,1,0:T(8,128)(2,1)S(1)}, bf16[4,16,1152]{2,1,0:T(8,128)(2,1)S(1)}, u32[]{:S(2)}, u32[]{:S(2)}) collective-permute-start(bf16[4,16,1152]{2,1,0:T(8,128)(2,1)S(1)} %get-tuple-element.45), channel_id=1, source_target_pairs={{0,4},{2,6},{4,0},{6,2},{8,12},{10,14},{12,8},{14,10},{16,20},{18,... | collective-permute-start | bytes 442376 | tf_op jit(solution)/shard_map/ppermute | solution.py:290
  77.3 7.8 %collective-permute-start.23 = (bf16[4,16,1152]{2,1,0:T(8,128)(2,1)S(1)}, bf16[4,16,1152]{2,1,0:T(8,128)(2,1)S(1)}, u32[]{:S(2)}, u32[]{:S(2)}) collective-permute-start(bf16[4,16,1152]{2,1,0:T(8,128)(2,1)S(1)} %get-tuple-element.46), channel_id=1, source_target_pairs={{0,6},{2,4},{4,2},{6,0},{8,14},{10,12},{12,10},{14,8},{16,22},{18,... | collective-permute-start | bytes 442376 | tf_op jit(solution)/shard_map/ppermute | solution.py:290
  85.2 4.5 %collective-permute-start.24 = (bf16[16,1152]{1,0:T(8,128)(2,1)S(1)}, bf16[16,1152]{1,0:T(8,128)(2,1)S(1)}, u32[]{:S(2)}, u32[]{:S(2)}) collective-permute-start(bf16[16,1152]{1,0:T(8,128)(2,1)S(1)} %get-tuple-element.48), channel_id=1, source_target_pairs={{0,8},{2,10},{4,12},{6,14},{8,0},{10,2},{12,4},{14,6},{16,24},{18,... | collective-permute-start | bytes 110600 | tf_op jit(solution)/shard_map/ppermute | solution.py:290
  85.3 4.9 %collective-permute-start.25 = (bf16[16,1152]{1,0:T(8,128)(2,1)S(1)}, bf16[16,1152]{1,0:T(8,128)(2,1)S(1)}, u32[]{:S(2)}, u32[]{:S(2)}) collective-permute-start(bf16[16,1152]{1,0:T(8,128)(2,1)S(1)} %get-tuple-element.49), channel_id=1, source_target_pairs={{0,16},{2,18},{4,20},{6,22},{8,24},{10,26},{12,28},{14,30},{16,0},... | collective-permute-start | bytes 110600 | tf_op jit(solution)/shard_map/ppermute | solution.py:290
  87.9 5.8 %collective-permute-start.26 = (bf16[16,1152]{1,0:T(8,128)(2,1)S(1)}, bf16[16,1152]{1,0:T(8,128)(2,1)S(1)}, u32[]{:S(2)}, u32[]{:S(2)}) collective-permute-start(bf16[16,1152]{1,0:T(8,128)(2,1)S(1)} %get-tuple-element.50), channel_id=1, source_target_pairs={{0,24},{2,26},{4,28},{6,30},{8,16},{10,18},{12,20},{14,22},{16,8},... | collective-permute-start | bytes 110600 | tf_op jit(solution)/shard_map/ppermute | solution.py:290
  106.2 1.3 collective-permute-start.27
  107.9 4.4 %collective-permute-start.28 = (bf16[16,1024]{1,0:T(8,128)(2,1)S(1)}, bf16[16,1024]{1,0:T(8,128)(2,1)S(1)}, u32[]{:S(2)}, u32[]{:S(2)}) collective-permute-start(bf16[16,1024]{1,0:T(8,128)(2,1)S(1)} %get-tuple-element.57), channel_id=1, source_target_pairs={{0,8},{2,10},{4,12},{6,14},{8,0},{10,2},{12,4},{14,6},{16,24},{18,... | collective-permute-start | bytes 98312 | tf_op jit(solution)/shard_map/ppermute | solution.py:290
  108.7 5.1 %collective-permute-start.29 = (bf16[16,1024]{1,0:T(8,128)(2,1)S(1)}, bf16[16,1024]{1,0:T(8,128)(2,1)S(1)}, u32[]{:S(2)}, u32[]{:S(2)}) collective-permute-start(bf16[16,1024]{1,0:T(8,128)(2,1)S(1)} %get-tuple-element.57), channel_id=1, source_target_pairs={{0,16},{2,18},{4,20},{6,22},{8,24},{10,26},{12,28},{14,30},{16,0},... | collective-permute-start | bytes 98312 | tf_op jit(solution)/shard_map/ppermute | solution.py:290
  110.3 5.7 %collective-permute-start.30 = (bf16[16,1024]{1,0:T(8,128)(2,1)S(1)}, bf16[16,1024]{1,0:T(8,128)(2,1)S(1)}, u32[]{:S(2)}, u32[]{:S(2)}) collective-permute-start(bf16[16,1024]{1,0:T(8,128)(2,1)S(1)} %get-tuple-element.57), channel_id=1, source_target_pairs={{0,24},{2,26},{4,28},{6,30},{8,16},{10,18},{12,20},{14,22},{16,8},... | collective-permute-start | bytes 98312 | tf_op jit(solution)/shard_map/ppermute | solution.py:290
  116.0 5.4 %collective-permute-start.31 = (bf16[4,16,1024]{2,1,0:T(8,128)(2,1)S(1)}, bf16[4,16,1024]{2,1,0:T(8,128)(2,1)S(1)}, u32[]{:S(2)}, u32[]{:S(2)}) collective-permute-start(bf16[4,16,1024]{2,1,0:T(8,128)(2,1)S(1)} %pad_maximum_fusion.2.refs_0_), channel_id=1, source_target_pairs={{0,2},{2,0},{4,6},{6,4},{8,10},{10,8},{12,14},{14,12},{16,18},{18,... | collective-permute-start | bytes 393224 | tf_op jit(solution)/shard_map/ppermute | solution.py:290
  116.7 5.3 %collective-permute-start.32 = (bf16[4,16,1024]{2,1,0:T(8,128)(2,1)S(1)}, bf16[4,16,1024]{2,1,0:T(8,128)(2,1)S(1)}, u32[]{:S(2)}, u32[]{:S(2)}) collective-permute-start(bf16[4,16,1024]{2,1,0:T(8,128)(2,1)S(1)} %pad_maximum_fusion.2.refs_0_), channel_id=1, source_target_pairs={{0,4},{2,6},{4,0},{6,2},{8,12},{10,14},{12,8},{14,10},{16,20},{18,... | collective-permute-start | bytes 393224 | tf_op jit(solution)/shard_map/ppermute | solution.py:290
  117.4 5.9 %collective-permute-start.33 = (bf16[4,16,1024]{2,1,0:T(8,128)(2,1)S(1)}, bf16[4,16,1024]{2,1,0:T(8,128)(2,1)S(1)}, u32[]{:S(2)}, u32[]{:S(2)}) collective-permute-start(bf16[4,16,1024]{2,1,0:T(8,128)(2,1)S(1)} %pad_maximum_fusion.2.refs_0_), channel_id=1, source_target_pairs={{0,6},{2,4},{4,2},{6,0},{8,14},{10,12},{12,10},{14,8},{16,22},{18,... | collective-permute-start | bytes 393224 | tf_op jit(solution)/shard_map/ppermute | solution.py:290
  124.5 1.2 collective-permute-start.34

commit v4 on v3

v4 whole, which is shorter than its diff:
```python
import math

import jax
import jax.numpy as jnp
from jax import lax
from jax.experimental import pallas as pl
from jax.experimental.pallas import tpu as pltpu
from jax.sharding import PartitionSpec as P

LANES = 128
SUBLANES = 8
LARGEST = 0.09375
HALF_RANGE = 60000.0


def split(values):
    high = values.astype(jnp.bfloat16)
    rest = values - high.astype(jnp.float32)
    middle = rest.astype(jnp.bfloat16)
    low = (rest - middle.astype(jnp.float32)).astype(jnp.bfloat16)
    return high, middle, low


def exact_dot(values, other, contract):
    rows = values.shape[0]
    product = lax.dot_general(
        jnp.concatenate(split(values), axis=0),
        other,
        (((1,), (contract,)), ((), ())),
        preferred_element_type=jnp.float32,
    )
    return product[:rows] + product[rows : 2 * rows] + product[2 * rows :]


def pack(*columns_in):
    rows = columns_in[0].shape[0]
    lane = lax.broadcasted_iota(jnp.int32, (rows, LANES), 1)
    tile = jnp.zeros((rows, LANES), jnp.float32)
    for place, column in enumerate(columns_in):
        for index, part in enumerate(split(column)):
            tile = jnp.where(lane == 3 * place + index, part.astype(jnp.float32), tile)
    return tile


def unpack(tile, place):
    return jnp.sum(tile[:, 3 * place : 3 * place + 3], axis=1, keepdims=True)


def wide(column):
    return jnp.broadcast_to(column, (column.shape[0], LANES))


def repeat(out_ref, block):
    for part in range(out_ref.shape[0]):
        out_ref[part] = block


def load_body(offsets_ref, design_ref, out_ref, sems):
    parts = offsets_ref.shape[0]
    width = design_ref.shape[1] // parts
    copies = []
    for part in range(parts):
        offset = pl.multiple_of(offsets_ref[part], width)
        copies.append(
            pltpu.make_async_copy(
                design_ref.at[:, pl.ds(offset, width)],
                out_ref.at[:, pl.ds(part * width, width)],
                sems.at[part],
            )
        )
    for copy in copies:
        copy.start()
    for copy in copies:
        copy.wait()


def rows_body(near, *refs):
    *field_refs, design_ref, extra_ref, out_ref = refs
    whole_refs, old_refs = field_refs[:near], field_refs[near:]
    rows, strengths, width = whole_refs[0].shape
    samples = design_ref.shape[0]
    total = jnp.zeros((strengths, samples), jnp.float32)
    squares = jnp.zeros((strengths, width), jnp.float32)
    products = jnp.zeros((strengths, width), jnp.float32)
    part = 0
    for index, whole_ref in enumerate(whole_refs):
        for row in range(rows):
            block = whole_ref[row]
            total += lax.dot_general(
                block,
                design_ref[:, part * width : (part + 1) * width],
                (((1,), (1,)), ((), ())),
                preferred_element_type=jnp.float32,
            )
            values = block.astype(jnp.float32)
            squares += values * values
            if old_refs:
                products += values * old_refs[index][row].astype(jnp.float32)
            part += 1
    out_ref[:, :samples] = total
    lane = lax.broadcasted_iota(jnp.int32, (strengths, LANES), 1)
    tile = extra_ref[...]
    if old_refs:
        tile = jnp.where(lane == 1, jnp.sum(products, axis=1, keepdims=True), tile)
    out_ref[:, samples:] = jnp.where(lane == 0, jnp.sum(squares, axis=1, keepdims=True), tile)


def columns(values, design_ref, out_refs, scale=None):
    rows = out_refs[0].shape[0]
    width = design_ref.shape[1] // (rows * len(out_refs))
    part = 0
    for out_ref in out_refs:
        for row in range(rows):
            block = lax.dot_general(
                values,
                design_ref[:, part * width : (part + 1) * width],
                (((1,), (0,)), ((), ())),
                preferred_element_type=jnp.float32,
            )
            if scale is not None:
                block = block * scale
            out_ref[row, :, :width] = block.astype(out_ref.dtype)
            part += 1


def miss_body(scale, both_ref, other_ref, labels_ref, design_ref, hessian_ref, *out_refs):
    samples = design_ref.shape[0]
    logits = both_ref[:, :samples] + other_ref[:, :samples]
    probability = 1.0 / (1.0 + jnp.exp(-logits))
    hessian_ref[...] = probability * (1.0 - probability)
    miss_rows = (probability - labels_ref[...].astype(jnp.float32)).astype(jnp.bfloat16)
    columns(miss_rows, design_ref, out_refs, scale)


def tile_of(*columns_in):
    rows = columns_in[0].shape[0]
    lane = lax.broadcasted_iota(jnp.int32, (rows, LANES), 1)
    tile = jnp.zeros((rows, LANES), jnp.float32)
    for place, column in enumerate(columns_in):
        tile = jnp.where(lane == place, column, tile)
    return tile


def dot_of(first, second):
    return jnp.sum(first * second, axis=1, keepdims=True)


def ratios_of(lam_ref, values_ref):
    lam = lam_ref[:, :1]
    values = values_ref[...]
    smallest = jnp.min(values, axis=1, keepdims=True)
    return (smallest + lam) / (values + lam) - 1.0


def gradient_body(summed_ref, weights_ref, lam_ref, sketch_ref, residual_ref, payload_ref):
    residual = -(summed_ref[...] + lam_ref[:, :1] * weights_ref[...])
    residual_ref[...] = residual
    repeat(payload_ref, exact_dot(residual, sketch_ref[...], 0).astype(jnp.bfloat16))


def first_body(
    summed_ref, other_ref, lam_ref, values_ref, sketch_ref, residual_ref,
    direction_ref, projected_ref, half_ref,
):
    projected = summed_ref[...] + other_ref[...]
    projected_ref[...] = projected
    scaled = ratios_of(lam_ref, values_ref) * projected
    direction = residual_ref[...] + exact_dot(scaled, sketch_ref[...], 1)
    direction_ref[...] = direction
    half_ref[...] = direction.astype(jnp.bfloat16)


def image_of(image_rows, hessian_ref):
    return (hessian_ref[...] * image_rows).astype(jnp.bfloat16)


def image_body(both_ref, other_ref, hessian_ref, design_ref, rows_ref, scalars_ref, *out_refs):
    samples = hessian_ref.shape[1]
    both = both_ref[...] + other_ref[...]
    image_rows = both[:, :samples]
    rows_ref[...] = image_rows
    image = image_of(image_rows, hessian_ref)
    scalars_ref[...] = tile_of(
        both[:, samples : samples + 1], dot_of(image.astype(jnp.float32), image_rows)
    )
    columns(image, design_ref, out_refs)


def fold_body(near, *refs):
    own_ref, *received_refs = refs[:near]
    kept_ref, *sent_refs = refs[near:]
    for row, target_ref in enumerate([kept_ref] + sent_refs):
        total = own_ref[row]
        for received_ref in received_refs:
            total += received_ref[row].astype(jnp.float32)
        target_ref[...] = total.astype(target_ref.dtype)


def image_project_body(far, *refs):
    kept_ref, *received_refs = refs[:far]
    scalars_ref, lam_ref, direction_ref, residual_ref, sketch_ref, applied_ref, payload_ref = refs[far:]
    rank = sketch_ref.shape[1]
    summed = kept_ref[...]
    for received_ref in received_refs:
        summed += received_ref[...].astype(jnp.float32)
    applied = summed + lam_ref[:, :1] * direction_ref[...]
    applied_ref[...] = applied
    projected = exact_dot(applied, sketch_ref[...], 0).astype(jnp.bfloat16)
    residual = residual_ref[...]
    packed = pack(scalars_ref[:, 1:2], dot_of(residual, residual)).astype(jnp.bfloat16)
    for part in range(payload_ref.shape[0]):
        payload_ref[part, :, :rank] = projected
        payload_ref[part, :, rank:] = packed


def second_body(
    summed_ref, other_ref, lam_ref, values_ref, sketch_ref, scalars_ref, projected_ref,
    weights_ref, direction_ref, residual_ref, applied_ref,
    precond_ref, update_ref, known_ref, extra_ref, half_ref,
):
    rank = sketch_ref.shape[1]
    lam = lam_ref[:, :1]
    ratios = ratios_of(lam_ref, values_ref)
    projected = projected_ref[...]
    square = unpack(summed_ref[:, rank:] + other_ref[:, rank:], 1)
    energy = unpack(summed_ref[:, rank:], 0)
    res_dot = square + dot_of(ratios * projected, projected)
    step_size = res_dot / (energy + lam * scalars_ref[:, :1])
    residual = residual_ref[...] - step_size * applied_ref[...]
    projected = projected - step_size * (summed_ref[:, :rank] + other_ref[:, :rank])
    scaled = ratios * projected
    precond_res = residual + exact_dot(scaled, sketch_ref[...], 1)
    precond_ref[...] = precond_res
    half_ref[...] = precond_res.astype(jnp.bfloat16)
    update_ref[...] = weights_ref[...] + step_size * direction_ref[...]
    known_ref[...] = tile_of(res_dot, dot_of(scaled, projected), energy, scalars_ref[:, :1])
    zero = jnp.zeros_like(square)
    extra_ref[...] = tile_of(zero, zero, dot_of(residual, residual))


def energy_body(both_ref, other_ref, hessian_ref, rows_ref, squares_ref, payload_ref):
    samples = hessian_ref.shape[1]
    both = both_ref[...] + other_ref[...]
    squares_ref[...] = both[:, samples:]
    image_rows = both[:, :samples]
    image = image_of(image_rows, hessian_ref).astype(jnp.float32)
    sums = [dot_of(image, image_rows), dot_of(image, rows_ref[...]), both[:, samples + 2 : samples + 3]]
    lane = lax.broadcasted_iota(jnp.int32, (SUBLANES, LANES), 1)
    tile = jnp.zeros((SUBLANES, LANES), jnp.float32)
    for group in range(both.shape[0] // SUBLANES):
        for place, column in enumerate(sums):
            piece = column[group * SUBLANES : (group + 1) * SUBLANES]
            tile = jnp.where(lane == len(sums) * group + place, piece, tile)
    repeat(payload_ref, tile)


def finish_body(
    received_ref, squares_ref, known_ref, lam_ref, precond_ref, direction_ref, update_ref, out_ref
):
    tile = received_ref[0]
    for part in range(1, received_ref.shape[0]):
        tile += received_ref[part]
    groups = direction_ref.shape[0] // SUBLANES

    def total(place):
        lanes = [3 * group + place for group in range(groups)]
        return jnp.concatenate([tile[:, lane : lane + 1] for lane in lanes], axis=0)

    old_dot, part, old_energy, old_square = (known_ref[:, lane : lane + 1] for lane in range(4))
    res_dot = total(2) + part
    beta = res_dot / old_dot
    energy = total(0) + beta * (2.0 * total(1) + beta * old_energy)
    square = squares_ref[:, :1] + beta * (2.0 * squares_ref[:, 1:2] + beta * old_square)
    step_size = res_dot / (energy + lam_ref[:, :1] * square)
    direction = precond_ref[...] + beta * direction_ref[...]
    out_ref[...] = update_ref[...] + step_size * direction


VMEM = pl.BlockSpec(memory_space=pltpu.VMEM)


def call(body, name, shapes, *operands):
    return pl.pallas_call(
        body,
        out_shape=[jax.ShapeDtypeStruct(shape, dtype) for shape, dtype in shapes],
        in_specs=[VMEM] * len(operands),
        out_specs=[VMEM] * len(shapes),
        compiler_params=pltpu.CompilerParams(vmem_limit_bytes=8 << 20),
        name=name,
    )(*operands)


def load(design, offsets):
    return pl.pallas_call(
        load_body,
        out_shape=pltpu.VMEM(design.shape, design.dtype),
        in_specs=[pl.BlockSpec(memory_space=pltpu.SMEM), pl.BlockSpec(memory_space=pltpu.HBM)],
        out_specs=VMEM,
        scratch_shapes=[pltpu.SemaphoreType.DMA((offsets.shape[0],))],
        compiler_params=pltpu.CompilerParams(vmem_limit_bytes=1 << 20),
        name="load",
    )(offsets, design)


def make_shards(samp, feat):
    near = min(samp, 4)
    far = samp // near
    near_order = list(range(1, near))
    far_order = sorted(range(1, far), key=lambda distance: (distance * 2) % (far + 1))

    def swap(values, distance):
        return lax.ppermute(values, "samp", [(i, i ^ distance) for i in range(samp)])

    def gather(block):
        column = jnp.stack([block] + [swap(block, near * distance) for distance in far_order])
        return [column] + [swap(column, distance) for distance in near_order]

    def exchange(blocks):
        return lax.all_to_all(blocks, "samp", 0, 0)

    def feat_parts(values):
        if feat == 2:
            return values, lax.ppermute(values, "feat", [(0, 1), (1, 0)])
        return lax.psum(values, "feat"), jnp.zeros_like(values)

    def shards(design_matrix, labels, weights, lambdas, sketch, sketch_values):
        strengths, width = weights.shape
        samples = design_matrix.shape[0]
        rank = sketch.shape[1]
        single, half = jnp.float32, jnp.bfloat16
        field = ((strengths, width), single)
        scalars = ((strengths, LANES), single)
        spread = ((strengths, width), half)
        payload = ((samp, strengths, rank), half)
        wide_payload = ((samp, strengths, rank + LANES), half)
        scale = 2.0 ** math.floor(math.log2(HALF_RANGE / (samples * near * LARGEST)))
        lam = jnp.broadcast_to(lambdas[:, None], (strengths, LANES))
        labels = labels[None, :]
        values = sketch_values[None, :]
        places = [k * near + j for j in [0] + near_order for k in [0] + far_order]
        places = jnp.bitwise_xor(lax.axis_index("samp"), jnp.array(places, jnp.int32))
        if width % LANES == 0:
            design = load(design_matrix, places * width)
        else:
            design = design_matrix.reshape(samples, samp, width)
            design = jnp.take(design, places, axis=1).reshape(design_matrix.shape)

        def apply_rows(fields, extra):
            shape = ((strengths, samples + LANES), single)
            return feat_parts(
                call(lambda *refs: rows_body(near, *refs), "rows", [shape], *fields, design, extra)[0]
            )

        def reduced(blocks):
            return feat_parts(jnp.sum(exchange(blocks).astype(single), axis=0))

        nothing = jnp.zeros((strengths, LANES), single)
        start = lax.optimization_barrier(weights.astype(half))
        hessian_diag, *outs = call(
            lambda *refs: miss_body(scale, *refs),
            "miss",
            [((strengths, samples), single)] + [((far, strengths, width), single)] * near,
            *apply_rows(gather(start), nothing), labels, design,
        )
        folded = outs[0]
        for index, distance in enumerate(near_order):
            folded = folded + swap(outs[index + 1].astype(jnp.float16), distance).astype(single)
        summed = folded[0]
        for index, distance in enumerate(far_order):
            part = folded[index + 1].astype(jnp.float16)
            summed = summed + swap(part, near * distance).astype(single)
        residual, blocks = call(
            gradient_body, "gradient", [field, payload], summed * (1.0 / scale), weights, lam, sketch
        )
        direction, projected, block = call(
            first_body, "first", [field, ((strengths, rank), single), spread],
            *reduced(blocks), lam, values, sketch, residual,
        )
        whole = gather(block)
        shape = (far, strengths, width)
        image_rows, known, *outs = call(
            image_body, "image",
            [((strengths, samples), single), scalars, (shape, single)] + [(shape, half)] * (near - 1),
            *apply_rows(whole, nothing), hessian_diag, design,
        )
        kept, *sent = call(
            lambda *refs: fold_body(near, *refs), "fold", [field] + [spread] * (far - 1),
            outs[0], *[swap(out, distance) for out, distance in zip(outs[1:], near_order)],
        )
        applied, blocks = call(
            lambda *refs: image_project_body(far, *refs), "project", [field, wide_payload],
            kept, *[swap(part, near * distance) for part, distance in zip(sent, far_order)],
            known, lam, direction, residual, sketch,
        )
        precond_res, update, known, extra, block = call(
            second_body, "second", [field, field, scalars, scalars, spread],
            *reduced(blocks), lam, values, sketch, known, projected,
            weights, direction, residual, applied,
        )
        squares, blocks = call(
            energy_body, "energy", [scalars, ((samp, SUBLANES, LANES), single)],
            *apply_rows(gather(block) + whole, extra), hessian_diag, image_rows,
        )
        return call(
            finish_body, "finish", [field],
            exchange(blocks), squares, known, lam, precond_res, direction, update,
        )[0]

    return shards


def solution(mesh):
    return jax.shard_map(
        make_shards(mesh.shape["samp"], mesh.shape["feat"]),
        mesh=mesh,
        in_specs=(
            P("samp", "feat"),
            P("samp"),
            P(None, ("feat", "samp")),
            P(),
            P(("feat", "samp"), None),
            P(),
        ),
        out_specs=P(None, ("feat", "samp")),
        check_vma=False,
    )
```

time: 139 us -> 136 us (0.978)
  waiting for transfers between devices: 45.6 us -> 43.4 us
    ppermute x30, waiting for transfers between devices: 39.6 us -> 37.5 us  [swap(): lax.ppermute(values, 'samp', [(i, i ^ distance) for i in range(samp)])]
  transfers between devices with their start and end apart: 35 -> 35, of which waited for: 25 -> 26; matrix products, arithmetic and copies ran while one was open for 1% -> 0% of each run, Pallas kernels for 1% -> 1%
where the time goes in v4:
time: 136 us; the launch traced here: 135 us
  waiting for transfers between devices  43.4 us (32%)
  starting transfers between devices  41.3 us (30%)
  blocking collectives  37.3 us (27%)
  Pallas kernels  8.82 us (6%)
  local copies, waits for them, and re-layouts  2.3 us (2%)
  other arithmetic  1.8 us (1%)
    ppermute x30, starting transfers between devices, swap(): lax.ppermute(values, 'samp', [(i, i ^ distance) for i in range(samp)])  41.1 us
    ppermute x30, waiting for transfers between devices, swap(): lax.ppermute(values, 'samp', [(i, i ^ distance) for i in range(samp)])  37.5 us
    all_to_all x3, blocking collectives, exchange(): return lax.all_to_all(blocks, 'samp', 0, 0)  37.3 us
    pallas_call x12, Pallas kernels, call(): pl.pallas_call(body, out_shape=[jax.ShapeDtypeStruct(shape, dtype) for sh...  7.78 us
    ppermute x5, waiting for transfers between devices, feat_parts(): return (values, lax.ppermute(values, 'feat', [(0, 1), (1, 0)]))  5.92 us
  transfers between devices with their start and end apart: 35, of which 26 were waited for; matrix products, arithmetic and copies ran while one was open for 0% of the time, Pallas kernels for 1%

profile of v4, /device:TPU:0, one launch (start us, length us, event | category | flops | bytes accessed | tf_op | source)
XLA Modules:
  0.0 135.2 jit_solution(4081091226904956782)
XLA Ops:
  0.8 4.1 %collective-permute-start.2 = (bf16[16,1024]{1,0:T(8,128)(2,1)S(1)}, bf16[16,1024]{1,0:T(8,128)(2,1)S(1)}, u32[]{:S(2)}, u32[]{:S(2)}) collective-permute-start(bf16[16,1024]{1,0:T(8,128)(2,1)S(1)} %convert_element_type.48), channel_id=1, source_target_pairs={{0,16},{2,18},{4,20},{6,22},{8,24},{10,26},{12,28},{14,30},{16,0},... | collective-permute-start | bytes 98312 | tf_op jit(solution)/shard_map/ppermute | solution.py:312
  4.9 1.6 %collective-permute-start.1 = (bf16[16,1024]{1,0:T(8,128)(2,1)S(1)}, bf16[16,1024]{1,0:T(8,128)(2,1)S(1)}, u32[]{:S(2)}, u32[]{:S(2)}) collective-permute-start(bf16[16,1024]{1,0:T(8,128)(2,1)S(1)} %convert_element_type.48), channel_id=1, source_target_pairs={{0,8},{2,10},{4,12},{6,14},{8,0},{10,2},{12,4},{14,6},{16,24},{18,... | collective-permute-start | bytes 98312 | tf_op jit(solution)/shard_map/ppermute | solution.py:312
  7.3 1.6 %collective-permute-done.1 = bf16[16,1024]{1,0:T(8,128)(2,1)S(1)} collective-permute-done((bf16[16,1024]{1,0:T(8,128)(2,1)S(1)}, bf16[16,1024]{1,0:T(8,128)(2,1)S(1)}, u32[]{:S(2)}, u32[]{:S(2)}) %collective-permute-start.1) | collective-permute-done | bytes 32800 | tf_op jit(solution)/shard_map/ppermute | solution.py:312
  8.8 3.4 %collective-permute-done = bf16[16,1024]{1,0:T(8,128)(2,1)S(1)} collective-permute-done((bf16[16,1024]{1,0:T(8,128)(2,1)S(1)}, bf16[16,1024]{1,0:T(8,128)(2,1)S(1)}, u32[]{:S(2)}, u32[]{:S(2)}) %collective-permute-start) | collective-permute-done | bytes 32800 | tf_op jit(solution)/shard_map/ppermute | solution.py:312
  12.2 2.5 %collective-permute-start.5 = (bf16[4,16,1024]{2,1,0:T(8,128)(2,1)S(1)}, bf16[4,16,1024]{2,1,0:T(8,128)(2,1)S(1)}, u32[]{:S(2)}, u32[]{:S(2)}) collective-permute-start(bf16[4,16,1024]{2,1,0:T(8,128)(2,1)S(1)} %pad_maximum_fusion.refs_0_), channel_id=1, source_target_pairs={{0,6},{2,4},{4,2},{6,0},{8,14},{10,12},{12,10},{14,8},{16,22},{18,... | collective-permute-start | bytes 393224 | tf_op jit(solution)/shard_map/ppermute | solution.py:312
  16.4 2.2 %copy-done.1 = bf16[128,16384]{1,0:T(8,128)(2,1)S(1)} copy-done((bf16[128,16384]{1,0:T(8,128)(2,1)S(1)}, bf16[128,16384]{1,0:T(8,128)(2,1)}, u32[]{:S(2)}) %copy-start.1) | copy-done | bytes 4194328
  18.6 1.0 load.1.refs_4_.refs_3_.design_ref.refs_8_
  20.3 1.2 rows.3.refs_0_
  21.6 1.2 collective-permute-done.6.refs_1_
  23.5 1.9 %collective-permute-start.9 = (f16[4,16,1024]{2,1,0:T(8,128)(2,1)S(1)}, f16[4,16,1024]{2,1,0:T(8,128)(2,1)S(1)}, u32[]{:S(2)}, u32[]{:S(2)}) collective-permute-start(f16[4,16,1024]{2,1,0:T(8,128)(2,1)S(1)} %convert_element_type.53), channel_id=1, source_target_pairs={{0,6},{2,4},{4,2},{6,0},{8,14},{10,12},{12,10},{14,8},{16,22},{18,... | collective-permute-start | bytes 393224 | tf_op jit(solution)/shard_map/ppermute | solution.py:312
  26.0 1.1 collective-permute-start.7
  27.1 3.8 %collective-permute-done.9 = f16[4,16,1024]{2,1,0:T(8,128)(2,1)S(1)} collective-permute-done((f16[4,16,1024]{2,1,0:T(8,128)(2,1)S(1)}, f16[4,16,1024]{2,1,0:T(8,128)(2,1)S(1)}, u32[]{:S(2)}, u32[]{:S(2)}) %collective-permute-start.9) | collective-permute-done | bytes 131104 | tf_op jit(solution)/shard_map/ppermute | solution.py:312
  30.9 2.0 %collective-permute-done.8 = f16[4,16,1024]{2,1,0:T(8,128)(2,1)S(1)} collective-permute-done((f16[4,16,1024]{2,1,0:T(8,128)(2,1)S(1)}, f16[4,16,1024]{2,1,0:T(8,128)(2,1)S(1)}, u32[]{:S(2)}, u32[]{:S(2)}) %collective-permute-start.8) | collective-permute-done | bytes 131104 | tf_op jit(solution)/shard_map/ppermute | solution.py:312
  33.5 4.0 %collective-permute-start.11 = (f16[16,1024]{1,0:T(8,128)(2,1)S(1)}, f16[16,1024]{1,0:T(8,128)(2,1)S(1)}, u32[]{:S(2)}, u32[]{:S(2)}) collective-permute-start(f16[16,1024]{1,0:T(8,128)(2,1)S(1)} %get-tuple-element.67), channel_id=1, source_target_pairs={{0,8},{2,10},{4,12},{6,14},{8,0},{10,2},{12,4},{14,6},{16,24},{18,... | collective-permute-start | bytes 98312 | tf_op jit(solution)/shard_map/ppermute | solution.py:312
  37.5 1.4 %collective-permute-done.10 = f16[16,1024]{1,0:T(8,128)(2,1)S(1)} collective-permute-done((f16[16,1024]{1,0:T(8,128)(2,1)S(1)}, f16[16,1024]{1,0:T(8,128)(2,1)S(1)}, u32[]{:S(2)}, u32[]{:S(2)}) %collective-permute-start.10) | collective-permute-done | bytes 32800 | tf_op jit(solution)/shard_map/ppermute | solution.py:312
  39.8 12.8 %all_to_all.15 = bf16[16,16,384]{2,1,0:T(8,128)(2,1)S(1)} all-to-all(bf16[16,16,384]{2,1,0:T(8,128)(2,1)S(1)} %get-tuple-element.38), channel_id=1, replica_groups=mesh['samp'=16,'feat'=2] {'samp'}, dimensions={0} | all-to-all | bytes 393216 | tf_op jit(solution)/shard_map/all_to_all | solution.py:319
  52.7 1.2 collective-permute-done.13.other_ref
  54.3 1.1 collective-permute-start.16
  55.4 1.1 collective-permute-start.15
  56.5 2.2 %collective-permute-start.14 = (bf16[16,1024]{1,0:T(8,128)(2,1)S(1)}, bf16[16,1024]{1,0:T(8,128)(2,1)S(1)}, u32[]{:S(2)}, u32[]{:S(2)}) collective-permute-start(bf16[16,1024]{1,0:T(8,128)(2,1)S(1)} %get-tuple-element.40), channel_id=1, source_target_pairs={{0,24},{2,26},{4,28},{6,30},{8,16},{10,18},{12,20},{14,22},{16,8},... | collective-permute-start | bytes 98312 | tf_op jit(solution)/shard_map/ppermute | solution.py:312
  59.6 2.6 %collective-permute-done.14 = bf16[16,1024]{1,0:T(8,128)(2,1)S(1)} collective-permute-done((bf16[16,1024]{1,0:T(8,128)(2,1)S(1)}, bf16[16,1024]{1,0:T(8,128)(2,1)S(1)}, u32[]{:S(2)}, u32[]{:S(2)}) %collective-permute-start.14) | collective-permute-done | bytes 32800 | tf_op jit(solution)/shard_map/ppermute | solution.py:312
  63.0 1.3 collective-permute-start.18
  64.3 1.5 %collective-permute-start.17 = (bf16[4,16,1024]{2,1,0:T(8,128)(2,1)S(1)}, bf16[4,16,1024]{2,1,0:T(8,128)(2,1)S(1)}, u32[]{:S(2)}, u32[]{:S(2)}) collective-permute-start(bf16[4,16,1024]{2,1,0:T(8,128)(2,1)S(1)} %pad_maximum_fusion.1.refs_0_.refs_4_), channel_id=1, source_target_pairs={{0,2},{2,0},{4,6},{6,4},{8,10},{10,8},{12,14},{14,12},{16,18},{18,... | collective-permute-start | bytes 393224 | tf_op jit(solution)/shard_map/ppermute | solution.py:312
  65.8 3.1 %collective-permute-done.19.refs_3_.refs_7_ = bf16[4,16,1024]{2,1,0:T(8,128)(2,1)S(1)} collective-permute-done((bf16[4,16,1024]{2,1,0:T(8,128)(2,1)S(1)}, bf16[4,16,1024]{2,1,0:T(8,128)(2,1)S(1)}, u32[]{:S(2)}, u32[]{:S(2)}) %collective-permute-start.19) | collective-permute-done | bytes 131104 | tf_op jit(solution)/shard_map/ppermute | solution.py:312
  69.7 1.2 rows.4.both_ref
  70.9 1.2 collective-permute-done.20.other_ref
  72.7 1.1 collective-permute-start.21
  74.7 1.6 %collective-permute-start.23 = (bf16[4,16,1024]{2,1,0:T(8,128)(2,1)S(1)}, bf16[4,16,1024]{2,1,0:T(8,128)(2,1)S(1)}, u32[]{:S(2)}, u32[]{:S(2)}) collective-permute-start(bf16[4,16,1024]{2,1,0:T(8,128)(2,1)S(1)} %get-tuple-element.45), channel_id=1, source_target_pairs={{0,6},{2,4},{4,2},{6,0},{8,14},{10,12},{12,10},{14,8},{16,22},{18,... | collective-permute-start | bytes 393224 | tf_op jit(solution)/shard_map/ppermute | solution.py:312
  76.3 2.9 %collective-permute-done.21.refs_1_ = bf16[4,16,1024]{2,1,0:T(8,128)(2,1)S(1)} collective-permute-done((bf16[4,16,1024]{2,1,0:T(8,128)(2,1)S(1)}, bf16[4,16,1024]{2,1,0:T(8,128)(2,1)S(1)}, u32[]{:S(2)}, u32[]{:S(2)}) %collective-permute-start.21) | collective-permute-done | bytes 131104 | tf_op jit(solution)/shard_map/ppermute | solution.py:312
  79.2 2.8 %collective-permute-done.22.refs_2_ = bf16[4,16,1024]{2,1,0:T(8,128)(2,1)S(1)} collective-permute-done((bf16[4,16,1024]{2,1,0:T(8,128)(2,1)S(1)}, bf16[4,16,1024]{2,1,0:T(8,128)(2,1)S(1)}, u32[]{:S(2)}, u32[]{:S(2)}) %collective-permute-start.22) | collective-permute-done | bytes 131104 | tf_op jit(solution)/shard_map/ppermute | solution.py:312
  82.0 2.6 %collective-permute-start.24 = (bf16[16,1024]{1,0:T(8,128)(2,1)S(1)}, bf16[16,1024]{1,0:T(8,128)(2,1)S(1)}, u32[]{:S(2)}, u32[]{:S(2)}) collective-permute-start(bf16[16,1024]{1,0:T(8,128)(2,1)S(1)} %get-tuple-element.47), channel_id=1, source_target_pairs={{0,24},{2,26},{4,28},{6,30},{8,16},{10,18},{12,20},{14,22},{16,8},... | collective-permute-start | bytes 98312 | tf_op jit(solution)/shard_map/ppermute | solution.py:312
  84.6 1.8 %collective-permute-start.26 = (bf16[16,1024]{1,0:T(8,128)(2,1)S(1)}, bf16[16,1024]{1,0:T(8,128)(2,1)S(1)}, u32[]{:S(2)}, u32[]{:S(2)}) collective-permute-start(bf16[16,1024]{1,0:T(8,128)(2,1)S(1)} %get-tuple-element.49), channel_id=1, source_target_pairs={{0,16},{2,18},{4,20},{6,22},{8,24},{10,26},{12,28},{14,30},{16,0},... | collective-permute-start | bytes 98312 | tf_op jit(solution)/shard_map/ppermute | solution.py:312
  86.4 1.3 collective-permute-done.24.refs_1_
  88.5 0.9 collective-permute-done.26.refs_3_
  89.7 12.5 %all_to_all.16 = bf16[16,16,512]{2,1,0:T(8,128)(2,1)S(1)} all-to-all(bf16[16,16,512]{2,1,0:T(8,128)(2,1)S(1)} %get-tuple-element.52), channel_id=1, replica_groups=mesh['samp'=16,'feat'=2] {'samp'}, dimensions={0} | all-to-all | bytes 524288 | tf_op jit(solution)/shard_map/all_to_all | solution.py:319
  102.3 1.2 collective-permute-done.27.other_ref
  104.1 1.1 collective-permute-start.30
  105.2 1.3 collective-permute-start.29
  106.5 2.0 %collective-permute-start.28 = (bf16[16,1024]{1,0:T(8,128)(2,1)S(1)}, bf16[16,1024]{1,0:T(8,128)(2,1)S(1)}, u32[]{:S(2)}, u32[]{:S(2)}) collective-permute-start(bf16[16,1024]{1,0:T(8,128)(2,1)S(1)} %get-tuple-element.55), channel_id=1, source_target_pairs={{0,24},{2,26},{4,28},{6,30},{8,16},{10,18},{12,20},{14,22},{16,8},... | collective-permute-start | bytes 98312 | tf_op jit(solution)/shard_map/ppermute | solution.py:312
  108.5 0.9 collective-permute-done.30
  109.5 2.7 %collective-permute-done.28 = bf16[16,1024]{1,0:T(8,128)(2,1)S(1)} collective-permute-done((bf16[16,1024]{1,0:T(8,128)(2,1)S(1)}, bf16[16,1024]{1,0:T(8,128)(2,1)S(1)}, u32[]{:S(2)}, u32[]{:S(2)}) %collective-permute-start.28) | collective-permute-done | bytes 32800 | tf_op jit(solution)/shard_map/ppermute | solution.py:312
  113.0 1.3 collective-permute-start.32
  114.3 1.5 %collective-permute-start.31 = (bf16[4,16,1024]{2,1,0:T(8,128)(2,1)S(1)}, bf16[4,16,1024]{2,1,0:T(8,128)(2,1)S(1)}, u32[]{:S(2)}, u32[]{:S(2)}) collective-permute-start(bf16[4,16,1024]{2,1,0:T(8,128)(2,1)S(1)} %pad_maximum_fusion.2.refs_0_), channel_id=1, source_target_pairs={{0,2},{2,0},{4,6},{6,4},{8,10},{10,8},{12,14},{14,12},{16,18},{18,... | collective-permute-start | bytes 393224 | tf_op jit(solution)/shard_map/ppermute | solution.py:312
  115.8 2.9 %collective-permute-done.33.refs_3_ = bf16[4,16,1024]{2,1,0:T(8,128)(2,1)S(1)} collective-permute-done((bf16[4,16,1024]{2,1,0:T(8,128)(2,1)S(1)}, bf16[4,16,1024]{2,1,0:T(8,128)(2,1)S(1)}, u32[]{:S(2)}, u32[]{:S(2)}) %collective-permute-start.33) | collective-permute-done | bytes 131104 | tf_op jit(solution)/shard_map/ppermute | solution.py:312
  119.5 1.2 rows.5.both_ref
  120.8 1.2 collective-permute-done.34.other_ref
  122.1 12.1 %all_to_all.17.received_ref = f32[16,8,128]{2,1,0:T(8,128)S(1)} all-to-all(f32[16,8,128]{2,1,0:T(8,128)S(1)} %get-tuple-element.58), channel_id=1, replica_groups=mesh['samp'=16,'feat'=2] {'samp'}, dimensions={0} | all-to-all | bytes 131072 | tf_op jit(solution)/shard_map/all_to_all | solution.py:319
  134.1 1.1 finish.1
  (66 shorter events, 15.0 us)
Async XLA Ops:
  0.8 6.4 %collective-permute-start.2 = (bf16[16,1024]{1,0:T(8,128)(2,1)S(1)}, bf16[16,1024]{1,0:T(8,128)(2,1)S(1)}, u32[]{:S(2)}, u32[]{:S(2)}) collective-permute-start(bf16[16,1024]{1,0:T(8,128)(2,1)S(1)} %convert_element_type.48), channel_id=1, source_target_pairs={{0,16},{2,18},{4,20},{6,22},{8,24},{10,26},{12,28},{14,30},{16,0},... | collective-permute-start | bytes 98312 | tf_op jit(solution)/shard_map/ppermute | solution.py:312
  4.9 3.9 %collective-permute-start.1 = (bf16[16,1024]{1,0:T(8,128)(2,1)S(1)}, bf16[16,1024]{1,0:T(8,128)(2,1)S(1)}, u32[]{:S(2)}, u32[]{:S(2)}) collective-permute-start(bf16[16,1024]{1,0:T(8,128)(2,1)S(1)} %convert_element_type.48), channel_id=1, source_target_pairs={{0,8},{2,10},{4,12},{6,14},{8,0},{10,2},{12,4},{14,6},{16,24},{18,... | collective-permute-start | bytes 98312 | tf_op jit(solution)/shard_map/ppermute | solution.py:312
  6.5 5.7 %collective-permute-start = (bf16[16,1024]{1,0:T(8,128)(2,1)S(1)}, bf16[16,1024]{1,0:T(8,128)(2,1)S(1)}, u32[]{:S(2)}, u32[]{:S(2)}) collective-permute-start(bf16[16,1024]{1,0:T(8,128)(2,1)S(1)} %convert_element_type.48), channel_id=1, source_target_pairs={{0,24},{2,26},{4,28},{6,30},{8,16},{10,18},{12,20},{14,22},{16,8},... | collective-permute-start | bytes 98312 | tf_op jit(solution)/shard_map/ppermute | solution.py:312
  12.2 7.5 %collective-permute-start.5 = (bf16[4,16,1024]{2,1,0:T(8,128)(2,1)S(1)}, bf16[4,16,1024]{2,1,0:T(8,128)(2,1)S(1)}, u32[]{:S(2)}, u32[]{:S(2)}) collective-permute-start(bf16[4,16,1024]{2,1,0:T(8,128)(2,1)S(1)} %pad_maximum_fusion.refs_0_), channel_id=1, source_target_pairs={{0,6},{2,4},{4,2},{6,0},{8,14},{10,12},{12,10},{14,8},{16,22},{18,... | collective-permute-start | bytes 393224 | tf_op jit(solution)/shard_map/ppermute | solution.py:312
  14.7 5.6 %collective-permute-start.4 = (bf16[4,16,1024]{2,1,0:T(8,128)(2,1)S(1)}, bf16[4,16,1024]{2,1,0:T(8,128)(2,1)S(1)}, u32[]{:S(2)}, u32[]{:S(2)}) collective-permute-start(bf16[4,16,1024]{2,1,0:T(8,128)(2,1)S(1)} %pad_maximum_fusion.refs_0_), channel_id=1, source_target_pairs={{0,4},{2,6},{4,0},{6,2},{8,12},{10,14},{12,8},{14,10},{16,20},{18,... | collective-permute-start | bytes 393224 | tf_op jit(solution)/shard_map/ppermute | solution.py:312
  15.2 5.1 %collective-permute-start.3 = (bf16[4,16,1024]{2,1,0:T(8,128)(2,1)S(1)}, bf16[4,16,1024]{2,1,0:T(8,128)(2,1)S(1)}, u32[]{:S(2)}, u32[]{:S(2)}) collective-permute-start(bf16[4,16,1024]{2,1,0:T(8,128)(2,1)S(1)} %pad_maximum_fusion.refs_0_), channel_id=1, source_target_pairs={{0,2},{2,0},{4,6},{6,4},{8,10},{10,8},{12,14},{14,12},{16,18},{18,... | collective-permute-start | bytes 393224 | tf_op jit(solution)/shard_map/ppermute | solution.py:312
  16.4 2.2 %copy-start.1 = (bf16[128,16384]{1,0:T(8,128)(2,1)S(1)}, bf16[128,16384]{1,0:T(8,128)(2,1)}, u32[]{:S(2)}) copy-start(bf16[128,16384]{1,0:T(8,128)(2,1)} %design_ref.1) | copy-start | bytes 12582916
  19.7 3.1 %copy-start.3 = (s32[128]{0:T(128)S(1)}, s32[128]{0:T(128)}, u32[]{:S(2)}) copy-start(s32[128]{0:T(128)} %param.8) | copy-start | bytes 1540
  21.5 17.9 %copy-start.5 = (f32[16]{0:T(128)S(1)}, f32[16]{0:T(128)}, u32[]{:S(2)}) copy-start(f32[16]{0:T(128)} %param.10) | copy-start | bytes 196
  21.5 17.9 %copy-start = (bf16[1024,384]{1,0:T(8,128)(2,1)S(1)}, bf16[1024,384]{1,0:T(8,128)(2,1)}, u32[]{:S(2)}) copy-start(bf16[1024,384]{1,0:T(8,128)(2,1)} %sketch_ref.5) | copy-start | bytes 2359300
  21.5 17.9 %copy-start.2 = (f32[16,1024]{1,0:T(8,128)S(1)}, f32[16,1024]{1,0:T(8,128)}, u32[]{:S(2)}) copy-start(f32[16,1024]{1,0:T(8,128)} %weights_ref.3) | copy-start | bytes 196612
  21.5 1.2 collective-permute-start.6
  22.8 29.9 %copy-start.4 = (f32[384]{0:T(512)S(1)}, f32[384]{0:T(512)}, u32[]{:S(2)}) copy-start(f32[384]{0:T(512)} %param.12) | copy-start | bytes 4612
  23.5 7.3 %collective-permute-start.9 = (f16[4,16,1024]{2,1,0:T(8,128)(2,1)S(1)}, f16[4,16,1024]{2,1,0:T(8,128)(2,1)S(1)}, u32[]{:S(2)}, u32[]{:S(2)}) collective-permute-start(f16[4,16,1024]{2,1,0:T(8,128)(2,1)S(1)} %convert_element_type.53), channel_id=1, source_target_pairs={{0,6},{2,4},{4,2},{6,0},{8,14},{10,12},{12,10},{14,8},{16,22},{18,... | collective-permute-start | bytes 393224 | tf_op jit(solution)/shard_map/ppermute | solution.py:312
  25.4 7.4 %collective-permute-start.8 = (f16[4,16,1024]{2,1,0:T(8,128)(2,1)S(1)}, f16[4,16,1024]{2,1,0:T(8,128)(2,1)S(1)}, u32[]{:S(2)}, u32[]{:S(2)}) collective-permute-start(f16[4,16,1024]{2,1,0:T(8,128)(2,1)S(1)} %convert_element_type.51), channel_id=1, source_target_pairs={{0,4},{2,6},{4,0},{6,2},{8,12},{10,14},{12,8},{14,10},{16,20},{18,... | collective-permute-start | bytes 393224 | tf_op jit(solution)/shard_map/ppermute | solution.py:312
  26.0 6.9 %collective-permute-start.7 = (f16[4,16,1024]{2,1,0:T(8,128)(2,1)S(1)}, f16[4,16,1024]{2,1,0:T(8,128)(2,1)S(1)}, u32[]{:S(2)}, u32[]{:S(2)}) collective-permute-start(f16[4,16,1024]{2,1,0:T(8,128)(2,1)S(1)} %convert_element_type.49), channel_id=1, source_target_pairs={{0,2},{2,0},{4,6},{6,4},{8,10},{10,8},{12,14},{14,12},{16,18},{18,... | collective-permute-start | bytes 393224 | tf_op jit(solution)/shard_map/ppermute | solution.py:312
  33.0 5.9 %collective-permute-start.10 = (f16[16,1024]{1,0:T(8,128)(2,1)S(1)}, f16[16,1024]{1,0:T(8,128)(2,1)S(1)}, u32[]{:S(2)}, u32[]{:S(2)}) collective-permute-start(f16[16,1024]{1,0:T(8,128)(2,1)S(1)} %get-tuple-element.65), channel_id=1, source_target_pairs={{0,24},{2,26},{4,28},{6,30},{8,16},{10,18},{12,20},{14,22},{16,8},... | collective-permute-start | bytes 98312 | tf_op jit(solution)/shard_map/ppermute | solution.py:312
  33.4 5.5 %collective-permute-start.12 = (f16[16,1024]{1,0:T(8,128)(2,1)S(1)}, f16[16,1024]{1,0:T(8,128)(2,1)S(1)}, u32[]{:S(2)}, u32[]{:S(2)}) collective-permute-start(f16[16,1024]{1,0:T(8,128)(2,1)S(1)} %get-tuple-element.66), channel_id=1, source_target_pairs={{0,16},{2,18},{4,20},{6,22},{8,24},{10,26},{12,28},{14,30},{16,0},... | collective-permute-start | bytes 98312 | tf_op jit(solution)/shard_map/ppermute | solution.py:312
  33.5 5.8 %collective-permute-start.11 = (f16[16,1024]{1,0:T(8,128)(2,1)S(1)}, f16[16,1024]{1,0:T(8,128)(2,1)S(1)}, u32[]{:S(2)}, u32[]{:S(2)}) collective-permute-start(f16[16,1024]{1,0:T(8,128)(2,1)S(1)} %get-tuple-element.67), channel_id=1, source_target_pairs={{0,8},{2,10},{4,12},{6,14},{8,0},{10,2},{12,4},{14,6},{16,24},{18,... | collective-permute-start | bytes 98312 | tf_op jit(solution)/shard_map/ppermute | solution.py:312
  52.6 1.3 collective-permute-start.13
  54.3 5.3 %collective-permute-start.16 = (bf16[16,1024]{1,0:T(8,128)(2,1)S(1)}, bf16[16,1024]{1,0:T(8,128)(2,1)S(1)}, u32[]{:S(2)}, u32[]{:S(2)}) collective-permute-start(bf16[16,1024]{1,0:T(8,128)(2,1)S(1)} %get-tuple-element.40), channel_id=1, source_target_pairs={{0,16},{2,18},{4,20},{6,22},{8,24},{10,26},{12,28},{14,30},{16,0},... | collective-permute-start | bytes 98312 | tf_op jit(solution)/shard_map/ppermute | solution.py:312
  55.4 4.2 %collective-permute-start.15 = (bf16[16,1024]{1,0:T(8,128)(2,1)S(1)}, bf16[16,1024]{1,0:T(8,128)(2,1)S(1)}, u32[]{:S(2)}, u32[]{:S(2)}) collective-permute-start(bf16[16,1024]{1,0:T(8,128)(2,1)S(1)} %get-tuple-element.40), channel_id=1, source_target_pairs={{0,8},{2,10},{4,12},{6,14},{8,0},{10,2},{12,4},{14,6},{16,24},{18,... | collective-permute-start | bytes 98312 | tf_op jit(solution)/shard_map/ppermute | solution.py:312
  56.5 5.7 %collective-permute-start.14 = (bf16[16,1024]{1,0:T(8,128)(2,1)S(1)}, bf16[16,1024]{1,0:T(8,128)(2,1)S(1)}, u32[]{:S(2)}, u32[]{:S(2)}) collective-permute-start(bf16[16,1024]{1,0:T(8,128)(2,1)S(1)} %get-tuple-element.40), channel_id=1, source_target_pairs={{0,24},{2,26},{4,28},{6,30},{8,16},{10,18},{12,20},{14,22},{16,8},... | collective-permute-start | bytes 98312 | tf_op jit(solution)/shard_map/ppermute | solution.py:312
  62.2 6.6 %collective-permute-start.19 = (bf16[4,16,1024]{2,1,0:T(8,128)(2,1)S(1)}, bf16[4,16,1024]{2,1,0:T(8,128)(2,1)S(1)}, u32[]{:S(2)}, u32[]{:S(2)}) collective-permute-start(bf16[4,16,1024]{2,1,0:T(8,128)(2,1)S(1)} %pad_maximum_fusion.1.refs_0_.refs_4_), channel_id=1, source_target_pairs={{0,6},{2,4},{4,2},{6,0},{8,14},{10,12},{12,10},{14,8},{16,22},{18,... | collective-permute-start | bytes 393224 | tf_op jit(solution)/shard_map/ppermute | solution.py:312
  63.0 6.7 %collective-permute-start.18 = (bf16[4,16,1024]{2,1,0:T(8,128)(2,1)S(1)}, bf16[4,16,1024]{2,1,0:T(8,128)(2,1)S(1)}, u32[]{:S(2)}, u32[]{:S(2)}) collective-permute-start(bf16[4,16,1024]{2,1,0:T(8,128)(2,1)S(1)} %pad_maximum_fusion.1.refs_0_.refs_4_), channel_id=1, source_target_pairs={{0,4},{2,6},{4,0},{6,2},{8,12},{10,14},{12,8},{14,10},{16,20},{18,... | collective-permute-start | bytes 393224 | tf_op jit(solution)/shard_map/ppermute | solution.py:312
  64.3 5.4 %collective-permute-start.17 = (bf16[4,16,1024]{2,1,0:T(8,128)(2,1)S(1)}, bf16[4,16,1024]{2,1,0:T(8,128)(2,1)S(1)}, u32[]{:S(2)}, u32[]{:S(2)}) collective-permute-start(bf16[4,16,1024]{2,1,0:T(8,128)(2,1)S(1)} %pad_maximum_fusion.1.refs_0_.refs_4_), channel_id=1, source_target_pairs={{0,2},{2,0},{4,6},{6,4},{8,10},{10,8},{12,14},{14,12},{16,18},{18,... | collective-permute-start | bytes 393224 | tf_op jit(solution)/shard_map/ppermute | solution.py:312
  70.9 1.2 collective-permute-start.20
  72.7 6.4 %collective-permute-start.21 = (bf16[4,16,1024]{2,1,0:T(8,128)(2,1)S(1)}, bf16[4,16,1024]{2,1,0:T(8,128)(2,1)S(1)}, u32[]{:S(2)}, u32[]{:S(2)}) collective-permute-start(bf16[4,16,1024]{2,1,0:T(8,128)(2,1)S(1)} %get-tuple-element.43), channel_id=1, source_target_pairs={{0,2},{2,0},{4,6},{6,4},{8,10},{10,8},{12,14},{14,12},{16,18},{18,... | collective-permute-start | bytes 393224 | tf_op jit(solution)/shard_map/ppermute | solution.py:312
  73.8 8.1 %collective-permute-start.22 = (bf16[4,16,1024]{2,1,0:T(8,128)(2,1)S(1)}, bf16[4,16,1024]{2,1,0:T(8,128)(2,1)S(1)}, u32[]{:S(2)}, u32[]{:S(2)}) collective-permute-start(bf16[4,16,1024]{2,1,0:T(8,128)(2,1)S(1)} %get-tuple-element.44), channel_id=1, source_target_pairs={{0,4},{2,6},{4,0},{6,2},{8,12},{10,14},{12,8},{14,10},{16,20},{18,... | collective-permute-start | bytes 393224 | tf_op jit(solution)/shard_map/ppermute | solution.py:312
  74.7 7.3 %collective-permute-start.23 = (bf16[4,16,1024]{2,1,0:T(8,128)(2,1)S(1)}, bf16[4,16,1024]{2,1,0:T(8,128)(2,1)S(1)}, u32[]{:S(2)}, u32[]{:S(2)}) collective-permute-start(bf16[4,16,1024]{2,1,0:T(8,128)(2,1)S(1)} %get-tuple-element.45), channel_id=1, source_target_pairs={{0,6},{2,4},{4,2},{6,0},{8,14},{10,12},{12,10},{14,8},{16,22},{18,... | collective-permute-start | bytes 393224 | tf_op jit(solution)/shard_map/ppermute | solution.py:312
  82.0 5.8 %collective-permute-start.24 = (bf16[16,1024]{1,0:T(8,128)(2,1)S(1)}, bf16[16,1024]{1,0:T(8,128)(2,1)S(1)}, u32[]{:S(2)}, u32[]{:S(2)}) collective-permute-start(bf16[16,1024]{1,0:T(8,128)(2,1)S(1)} %get-tuple-element.47), channel_id=1, source_target_pairs={{0,24},{2,26},{4,28},{6,30},{8,16},{10,18},{12,20},{14,22},{16,8},... | collective-permute-start | bytes 98312 | tf_op jit(solution)/shard_map/ppermute | solution.py:312
  84.6 3.9 %collective-permute-start.25 = (bf16[16,1024]{1,0:T(8,128)(2,1)S(1)}, bf16[16,1024]{1,0:T(8,128)(2,1)S(1)}, u32[]{:S(2)}, u32[]{:S(2)}) collective-permute-start(bf16[16,1024]{1,0:T(8,128)(2,1)S(1)} %get-tuple-element.48), channel_id=1, source_target_pairs={{0,8},{2,10},{4,12},{6,14},{8,0},{10,2},{12,4},{14,6},{16,24},{18,... | collective-permute-start | bytes 98312 | tf_op jit(solution)/shard_map/ppermute | solution.py:312
  84.6 4.8 %collective-permute-start.26 = (bf16[16,1024]{1,0:T(8,128)(2,1)S(1)}, bf16[16,1024]{1,0:T(8,128)(2,1)S(1)}, u32[]{:S(2)}, u32[]{:S(2)}) collective-permute-start(bf16[16,1024]{1,0:T(8,128)(2,1)S(1)} %get-tuple-element.49), channel_id=1, source_target_pairs={{0,16},{2,18},{4,20},{6,22},{8,24},{10,26},{12,28},{14,30},{16,0},... | collective-permute-start | bytes 98312 | tf_op jit(solution)/shard_map/ppermute | solution.py:312
  102.3 1.3 collective-permute-start.27
  104.1 5.4 %collective-permute-start.30 = (bf16[16,1024]{1,0:T(8,128)(2,1)S(1)}, bf16[16,1024]{1,0:T(8,128)(2,1)S(1)}, u32[]{:S(2)}, u32[]{:S(2)}) collective-permute-start(bf16[16,1024]{1,0:T(8,128)(2,1)S(1)} %get-tuple-element.55), channel_id=1, source_target_pairs={{0,16},{2,18},{4,20},{6,22},{8,24},{10,26},{12,28},{14,30},{16,0},... | collective-permute-start | bytes 98312 | tf_op jit(solution)/shard_map/ppermute | solution.py:312
  105.2 4.2 %collective-permute-start.29 = (bf16[16,1024]{1,0:T(8,128)(2,1)S(1)}, bf16[16,1024]{1,0:T(8,128)(2,1)S(1)}, u32[]{:S(2)}, u32[]{:S(2)}) collective-permute-start(bf16[16,1024]{1,0:T(8,128)(2,1)S(1)} %get-tuple-element.55), channel_id=1, source_target_pairs={{0,8},{2,10},{4,12},{6,14},{8,0},{10,2},{12,4},{14,6},{16,24},{18,... | collective-permute-start | bytes 98312 | tf_op jit(solution)/shard_map/ppermute | solution.py:312
  106.5 5.7 %collective-permute-start.28 = (bf16[16,1024]{1,0:T(8,128)(2,1)S(1)}, bf16[16,1024]{1,0:T(8,128)(2,1)S(1)}, u32[]{:S(2)}, u32[]{:S(2)}) collective-permute-start(bf16[16,1024]{1,0:T(8,128)(2,1)S(1)} %get-tuple-element.55), channel_id=1, source_target_pairs={{0,24},{2,26},{4,28},{6,30},{8,16},{10,18},{12,20},{14,22},{16,8},... | collective-permute-start | bytes 98312 | tf_op jit(solution)/shard_map/ppermute | solution.py:312
  112.2 6.5 %collective-permute-start.33 = (bf16[4,16,1024]{2,1,0:T(8,128)(2,1)S(1)}, bf16[4,16,1024]{2,1,0:T(8,128)(2,1)S(1)}, u32[]{:S(2)}, u32[]{:S(2)}) collective-permute-start(bf16[4,16,1024]{2,1,0:T(8,128)(2,1)S(1)} %pad_maximum_fusion.2.refs_0_), channel_id=1, source_target_pairs={{0,6},{2,4},{4,2},{6,0},{8,14},{10,12},{12,10},{14,8},{16,22},{18,... | collective-permute-start | bytes 393224 | tf_op jit(solution)/shard_map/ppermute | solution.py:312
  113.0 6.5 %collective-permute-start.32 = (bf16[4,16,1024]{2,1,0:T(8,128)(2,1)S(1)}, bf16[4,16,1024]{2,1,0:T(8,128)(2,1)S(1)}, u32[]{:S(2)}, u32[]{:S(2)}) collective-permute-start(bf16[4,16,1024]{2,1,0:T(8,128)(2,1)S(1)} %pad_maximum_fusion.2.refs_0_), channel_id=1, source_target_pairs={{0,4},{2,6},{4,0},{6,2},{8,12},{10,14},{12,8},{14,10},{16,20},{18,... | collective-permute-start | bytes 393224 | tf_op jit(solution)/shard_map/ppermute | solution.py:312
  114.3 5.2 %collective-permute-start.31 = (bf16[4,16,1024]{2,1,0:T(8,128)(2,1)S(1)}, bf16[4,16,1024]{2,1,0:T(8,128)(2,1)S(1)}, u32[]{:S(2)}, u32[]{:S(2)}) collective-permute-start(bf16[4,16,1024]{2,1,0:T(8,128)(2,1)S(1)} %pad_maximum_fusion.2.refs_0_), channel_id=1, source_target_pairs={{0,2},{2,0},{4,6},{6,4},{8,10},{10,8},{12,14},{14,12},{16,18},{18,... | collective-permute-start | bytes 393224 | tf_op jit(solution)/shard_map/ppermute | solution.py:312
  120.8 1.2 collective-permute-start.34
